TPU v7x, 128 devices: a whole 4x4x4 slice. The times are simulated.
128 devices in a mesh: grp: 16 (over y, x), col: 8 (over z, core).
Axes of the slice: x: 4, y: 4, z: 4, core: 2. Of those that a mesh axis runs over, the one named last changes fastest.
Arguments:
- front: float32 [16384, 16384], P(None, ('grp', 'col')), as said below
- contributions: float32 [16, 1024, 1024], P('grp', None, 'col')
- block_map: int32 [16, 8], P('grp'), may hold values from 0 to 127, as said below
- pivot_flags: int32 [16384], P(('grp', 'col')), may hold values 0 or 1
Outputs:
- factored: float32 [16384, 16384], P(None, ('grp', 'col'))
Inputs may be any that keep to these rules, and one draw needn't show every extreme that they name: `block_map`: within each child the 8 entries are distinct, and entry j leaves the remainder j when divided by 8. The assembled front is symmetric positive definite.
All inputs are finite; a program needn't handle non-finite values. No bound on the sum of `pivot_flags` on one device may be relied on, other than what follows from the above.
Results may differ from a plain program's by a relative error of at most 0.005.
Values may be sent and summed in bfloat16 or wider, within the bound.
A program may use at most 192 MiB of HBM per device.

v0:
```python
import jax
import jax.numpy as jnp
from jax import lax
from jax.sharding import PartitionSpec as P

PANELS = 4


def spread(value, axis, source):
    kept = jnp.where(lax.axis_index(axis) == source, value, 0).astype(value.dtype)
    return lax.psum(kept, axis)


def factor_panel(column, earlier, pivots, step, width):
    if step > 0:
        rows = (
            earlier[step * width : (step + 1) * width].astype(jnp.float32)
            * pivots.astype(jnp.float32)[None, :]
        )
        coef = rows.astype(jnp.bfloat16)
        column = column - lax.dot_general(
            earlier, coef, (((1,), (1,)), ((), ())), preferred_element_type=jnp.float32
        )
    block = column[step * width : (step + 1) * width]
    chol = jnp.linalg.cholesky(block)
    cdiag = jnp.diagonal(chol)
    below = column[(step + 1) * width :]
    lower = (
        lax.linalg.triangular_solve(chol, below, left_side=False, lower=True, transpose_a=True)
        / cdiag[None, :]
    )
    unit = chol / cdiag[None, :]
    upper = jnp.zeros((step * width, width), jnp.float32)
    panel = jnp.concatenate([upper, unit, lower], axis=0).astype(jnp.bfloat16)
    return (panel, (cdiag * cdiag).astype(jnp.bfloat16))


def trailing_update(total, lcols, lpivots, owner, width):
    rows = lax.dynamic_slice_in_dim(lcols, owner * width, width, 0).astype(jnp.float32)
    coef = (rows * lpivots.astype(jnp.float32)[None, :]).astype(jnp.bfloat16)
    return total - lax.dot_general(
        lcols, coef, (((1,), (1,)), ((), ())), preferred_element_type=jnp.float32
    )


def on_device(front, contributions, block_map, pivot_flags):
    order = front.shape[0]
    width = front.shape[1]
    blocks = order // width
    child = contributions.shape[1]
    share = contributions.shape[2] // width
    owner = lax.axis_index(("grp", "col"))
    col_id = lax.axis_index("col")
    parts = lax.all_gather(contributions, "grp", axis=0, tiled=True)
    maps = lax.all_gather(block_map, "grp", axis=0, tiled=True)
    count = parts.shape[0]
    own = lax.dynamic_slice_in_dim(maps, col_id * share, share, 1)
    pick = (own == owner).astype(jnp.float32)
    chosen = jnp.einsum(
        "kj,krjb->krb",
        pick,
        parts.reshape(count, child, share, width),
        precision=lax.Precision.HIGHEST,
    )
    chosen = chosen.reshape(count * (child // width), width, width)
    tiles = front.reshape(blocks, width, width).at[maps.reshape(-1)].add(chosen)
    assembled = tiles.reshape(order, width)
    inner = jnp.arange(width, dtype=jnp.int32)
    assembled = assembled.at[owner * width + inner, inner].add(pivot_flags.astype(jnp.float32))
    panels = []
    pivots = []
    total = assembled
    for step in range(PANELS):
        if step > 0:
            earlier = jnp.concatenate(panels, axis=1)
            before = jnp.concatenate(pivots)
        else:
            earlier = jnp.zeros((order, 0), jnp.bfloat16)
            before = jnp.zeros((0,), jnp.bfloat16)
        candidate = factor_panel(assembled, earlier, before, step, width)
        got_l, got_d = (
            spread(candidate[0], ("grp", "col"), step),
            spread(candidate[1], ("grp", "col"), step),
        )
        panels.append(got_l)
        pivots.append(got_d)
    all_l = jnp.concatenate(panels, axis=1)
    all_d = jnp.concatenate(pivots)
    total = trailing_update(total, all_l, all_d, owner, width)
    keep = (jnp.arange(order, dtype=jnp.int32) >= PANELS * width)[:, None]
    trailing = jnp.where(keep, total, 0.0)
    own_l = lax.dynamic_slice_in_dim(
        all_l, jnp.minimum(owner, PANELS - 1) * width, width, 1
    ).astype(jnp.float32)
    return jnp.where(owner < PANELS, own_l, trailing)


def solution(mesh):
    return jax.shard_map(
        on_device,
        mesh=mesh,
        in_specs=(
            P(None, ("grp", "col")),
            P("grp", None, "col"),
            P("grp", None),
            P(("grp", "col")),
        ),
        out_specs=P(None, ("grp", "col")),
        check_vma=False,
    )
```

profile of v0, /device:TPU:9, one launch (start us, length us, event | category | flops | bytes accessed | tf_op | source)
XLA Modules:
  0.0 1023.5 jit_solution(4497614284063848112)
XLA Ops:
  12.5 16.0 %all-gather = s32[16,1,8]{2,1,0:T(1,128)S(1)} all-gather(s32[1,1,8]{2,1,0:T(1,128)S(1)} %bitcast.53), channel_id=1, replica_groups=mesh['grp'=16,'col'=8] {'grp'}, dimensions={0}, use_global_device_ids=true | all-gather | bytes 544 | tf_op jit(solution)/shard_map/all_gather | solution.py:55
  30.0 55.3 %all-gather.3.cloned.1.call-done = f32[16,1024,128]{2,1,0:T(8,128)} async-done(((f32[1,1024,128]{2,1,0:T(8,128)}), f32[16,1024,128]{2,1,0:T(8,128)}) %all-gather.3.cloned.1.call-update) | async-done | bytes 8388624 | tf_op jit(solution)/shard_map/all_gather | solution.py:54
  92.8 26.4 %scatter_fusion = f32[128,128,128]{2,1,0:T(8,128)} fusion(f32[128,128,128]{2,1,0:T(8,128)} %bitcast.50, s32[128]{0:T(128)S(1)} %fusion.43, f32[128,128,128]{2,1,0:T(8,128)} %bitcast.52), kind=kCustom, calls=%fused_computation.4 | custom fusion | flops 2097152 | bytes 25166336 | tf_op jit(solution)/shard_map/scatter-add | solution.py:66
  119.2 17.9 %scatter_fusion.1 = f32[16384,128]{1,0:T(8,128)} fusion(f32[16384,128]{1,0:T(8,128)} %bitcast.51, s32[128]{0:T(128)S(1)} %get-tuple-element.23, f32[128]{0:T(128)S(1)} %convert_element_type.81), kind=kCustom, calls=%fused_computation.5 | custom fusion | flops 128 | bytes 2560 | tf_op jit(solution)/shard_map/scatter-add | solution.py:69
  147.9 11.7 %cholesky.74 = f32[128,128]{1,0:T(8,128)S(1)} custom-call(f32[128,128]{1,0:T(8,128)S(1)} %fusion.22), custom_call_target="Cholesky" | custom-call | tf_op jit(solution)/shard_map/jit(cholesky)/cholesky | solution.py:25
  183.6 65.3 %psum.57 = bf16[128]{0:T(256)(128)(2,1)S(1)} all-reduce(bf16[128]{0:T(256)(128)(2,1)S(1)} %broadcast_select_fusion.3), channel_id=1, replica_groups=mesh['grp'=16,'col'=8] {'grp','col'}, use_global_device_ids=true, to_apply=%region_5.7 | all-reduce | flops 128 | bytes 512 | tf_op jit(solution)/shard_map/psum | solution.py:11
  248.8 88.1 %all-reduce.5.cloned.1.call-done = bf16[16384,128]{1,0:T(8,128)(2,1)} async-done(((bf16[16384,128]{1,0:T(8,128)(2,1)}), bf16[16384,128]{1,0:T(8,128)(2,1)}) %all-reduce.5.cloned.1.call-update) | async-done | bytes 4194320 | tf_op jit(solution)/shard_map/psum | solution.py:11
  347.1 11.7 %cholesky.85 = f32[128,128]{1,0:T(8,128)S(1)} custom-call(f32[128,128]{1,0:T(8,128)S(1)} %fusion.20), custom_call_target="Cholesky" | custom-call | tf_op jit(solution)/shard_map/jit(cholesky)/cholesky | solution.py:25
  371.2 15.2 %fusion.4 = bf16[16128,128]{1,0:T(8,128)(2,1)S(1)} fusion(f32[16384,128]{0,1:T(8,128)} %copy-done, f32[128]{0:T(128)S(1)} %gather_fusion.1, f32[1,128,128]{1,2,0:T(8,128)S(1)} %custom-call.15), kind=kOutput, calls=%fused_computation.17 | convolution fusion | flops 3175022592 | bytes 12452352 | tf_op jit(solution)/shard_map/triangular_solve | solution.py:29
  386.4 10.5 %maximum_select_fusion.1 = bf16[16384,128]{1,0:T(8,128)(2,1)} fusion(bf16[16128,128]{1,0:T(8,128)(2,1)S(1)} %fusion.4, bf16[128,128]{1,0:T(8,128)(2,1)S(1)} %divide_convert_fusion.2, pred[]{:T(512)S(6)} %eq.25, bf16[16384]{0:T(1024)(128)(2,1)S(1)} %pad.15.clone), kind=kLoop, calls=%fused_computation.25 | loop fusion | flops 14680064 | bytes 8388609 | tf_op jit(solution)/shard_map/jit(_where)/select_n | solution.py:10
  397.0 65.2 %psum.59 = bf16[128]{0:T(256)(128)(2,1)S(1)} all-reduce(bf16[128]{0:T(256)(128)(2,1)S(1)} %broadcast_select_fusion.2), channel_id=1, replica_groups=mesh['grp'=16,'col'=8] {'grp','col'}, use_global_device_ids=true, to_apply=%region_7.9 | all-reduce | flops 128 | bytes 512 | tf_op jit(solution)/shard_map/psum | solution.py:11
  469.1 80.8 %all-reduce.7.cloned.1.call-done = bf16[16384,128]{1,0:T(8,128)(2,1)} async-done(((bf16[16384,128]{1,0:T(8,128)(2,1)}), bf16[16384,128]{1,0:T(8,128)(2,1)}) %all-reduce.7.cloned.1.call-update) | async-done | bytes 4194320 | tf_op jit(solution)/shard_map/psum | solution.py:11
  569.5 11.7 %cholesky.96 = f32[128,128]{1,0:T(8,128)S(1)} custom-call(f32[128,128]{1,0:T(8,128)S(1)} %fusion.18), custom_call_target="Cholesky" | custom-call | tf_op jit(solution)/shard_map/jit(cholesky)/cholesky | solution.py:25
  593.7 15.4 %fusion.3 = bf16[16000,128]{1,0:T(8,128)(2,1)S(1)} fusion(f32[16384,128]{0,1:T(8,128)} %copy-done.2, f32[128]{0:T(128)S(1)} %gather_fusion.2, f32[1,128,128]{1,2,0:T(8,128)S(1)} %custom-call.16), kind=kOutput, calls=%fused_computation.15 | convolution fusion | flops 3149824000 | bytes 12354048 | tf_op jit(solution)/shard_map/triangular_solve | solution.py:29
  609.1 11.3 %maximum_select_fusion.2 = bf16[16384,128]{1,0:T(8,128)(2,1)} fusion(bf16[16000,128]{1,0:T(8,128)(2,1)S(1)} %fusion.3, bf16[128,128]{1,0:T(8,128)(2,1)S(1)} %divide_convert_fusion.1, pred[]{:T(512)S(6)} %eq.26, bf16[16384]{0:T(1024)(128)(2,1)S(1)} %pad.10.clone), kind=kLoop, calls=%fused_computation.26 | loop fusion | flops 14680064 | bytes 8355841 | tf_op jit(solution)/shard_map/jit(_where)/select_n | solution.py:10
  620.5 65.3 %psum.61 = bf16[128]{0:T(256)(128)(2,1)S(1)} all-reduce(bf16[128]{0:T(256)(128)(2,1)S(1)} %broadcast_select_fusion.1), channel_id=1, replica_groups=mesh['grp'=16,'col'=8] {'grp','col'}, use_global_device_ids=true, to_apply=%region_9.11 | all-reduce | flops 128 | bytes 512 | tf_op jit(solution)/shard_map/psum | solution.py:11
  685.8 87.6 %all-reduce.9.cloned.1.call-done = bf16[16384,128]{1,0:T(8,128)(2,1)} async-done(((bf16[16384,128]{1,0:T(8,128)(2,1)}), bf16[16384,128]{1,0:T(8,128)(2,1)}) %all-reduce.9.cloned.1.call-update) | async-done | bytes 4194320 | tf_op jit(solution)/shard_map/psum | solution.py:11
  778.7 11.0 %convolution_subtract_fusion.3 = f32[16384,128]{0,1:T(8,128)S(1)} fusion(f32[16384,128]{0,1:T(8,128)} %copy.27, bf16[16384,384]{1,0:T(8,128)(2,1)} %get-tuple-element.14, f32[384]{0:T(512)S(1)} %maximum_convert_fusion), kind=kOutput, calls=%fused_computation.9 | convolution fusion | flops 1612857344 | bytes 29459968 | tf_op jit(solution)/shard_map/dot_general | solution.py:21
  793.9 11.7 %cholesky.107 = f32[128,128]{1,0:T(8,128)S(1)} custom-call(f32[128,128]{1,0:T(8,128)S(1)} %fusion.16), custom_call_target="Cholesky" | custom-call | tf_op jit(solution)/shard_map/jit(cholesky)/cholesky | solution.py:25
  818.0 15.2 %fusion.2 = bf16[15872,128]{1,0:T(8,128)(2,1)S(1)} fusion(f32[16384,128]{0,1:T(8,128)} %copy-done.1, f32[128]{0:T(128)S(1)} %gather_fusion.3, f32[1,128,128]{1,2,0:T(8,128)S(1)} %custom-call.17), kind=kOutput, calls=%fused_computation.13 | convolution fusion | flops 3124625408 | bytes 12255744 | tf_op jit(solution)/shard_map/triangular_solve | solution.py:29
  833.3 12.1 %maximum_select_fusion.3 = bf16[16384,128]{1,0:T(8,128)(2,1)} fusion(bf16[15872,128]{1,0:T(8,128)(2,1)S(1)} %fusion.2, bf16[128,128]{1,0:T(8,128)(2,1)S(1)} %divide_convert_fusion, pred[]{:T(512)S(6)} %eq.27, bf16[16384]{0:T(1024)(128)(2,1)S(1)} %pad.4.clone), kind=kLoop, calls=%fused_computation.27 | loop fusion | flops 14680064 | bytes 8323073 | tf_op jit(solution)/shard_map/jit(_where)/select_n | solution.py:10
  845.4 65.0 %psum.63 = bf16[128]{0:T(256)(128)(2,1)S(1)} all-reduce(bf16[128]{0:T(256)(128)(2,1)S(1)} %broadcast_select_fusion), channel_id=1, replica_groups=mesh['grp'=16,'col'=8] {'grp','col'}, use_global_device_ids=true, to_apply=%region_11.13 | all-reduce | flops 128 | bytes 512 | tf_op jit(solution)/shard_map/psum | solution.py:11
  910.4 87.9 %all-reduce.11.cloned.1.call-done = bf16[16384,128]{1,0:T(8,128)(2,1)} async-done(((bf16[16384,128]{1,0:T(8,128)(2,1)}), bf16[16384,128]{1,0:T(8,128)(2,1)}) %all-reduce.11.cloned.1.call-update) | async-done | bytes 4194320 | tf_op jit(solution)/shard_map/psum | solution.py:11
  1002.2 14.3 %fusion.1 = f32[16384,128]{1,0:T(8,128)} fusion(f32[16384,128]{1,0:T(8,128)} %scatter_fusion.1, bf16[16384,512]{1,0:T(8,128)(2,1)} %constant_dynamic-update-slice_fusion.5, s32[]{:T(128)S(6)} %select_n.125, pred[16384]{0:T(1024)(128)(4,1)S(1)} %iota_compare_fusion.2, pred[]{:T(512)S(6)} %lt.43, f32[512]{0:T(512)S(1)} %maximum_convert_fusion.1, ...), kind=kOutput, calls=%fused_computation.11 | convolution fusion | flops 2156068864 | bytes 37898248 | tf_op jit(solution)/shard_map/dot_general | solution.py:41
  (89 shorter events, 136.8 us)
Async XLA Ops:
  6.5 6.0 copy-start.3
  6.5 23.2 %copy-start.4 = (s32[128]{0:T(128)S(1)}, s32[128]{0:T(128)}, u32[]{:S(2)}) copy-start(s32[128]{0:T(128)} %param.8) | copy-start | bytes 1540
  6.5 78.8 %all-gather.3.cloned.1.call-start = ((), (), s32[]{:S(2)}) async-start(), calls=%async_computation | async-start | bytes 8912896 | tf_op jit(solution)/shard_map/all_gather | solution.py:54
  12.4 324.5 %all-reduce.5.cloned.1.call-start = ((), (), s32[]{:S(2)}) async-start(), calls=%async_computation.1 | async-start | bytes 8388608 | tf_op jit(solution)/shard_map/psum | solution.py:11
  183.4 366.5 %all-reduce.7.cloned.1.call-start = ((), (), s32[]{:S(2)}) async-start(), calls=%async_computation.2 | async-start | bytes 8388608 | tf_op jit(solution)/shard_map/psum | solution.py:11
  342.9 3.2 copy-start
  396.9 376.5 %all-reduce.9.cloned.1.call-start = ((), (), s32[]{:S(2)}) async-start(), calls=%async_computation.3 | async-start | bytes 8388608 | tf_op jit(solution)/shard_map/psum | solution.py:11
  565.4 3.2 copy-start.2
  620.4 377.9 %all-reduce.11.cloned.1.call-start = ((), (), s32[]{:S(2)}) async-start(), calls=%async_computation.4 | async-start | bytes 8388608 | tf_op jit(solution)/shard_map/psum | solution.py:11
  789.7 3.2 copy-start.1
Sparse Core Ops, SparseCore 0:
  12.6 72.7 all-gather.2
  183.6 153.3 all-reduce.4
  397.1 152.8 all-reduce.6
  620.5 152.8 all-reduce.8
  845.5 152.7 all-reduce.10
where the time goes:
time: 1040 us; the launch traced here: 1020 us
  waiting for transfers between devices  400 us (38%)
  blocking collectives  277 us (27%)
  other arithmetic  184 us (18%)
  matrix products  94.5 us (9%)
  local copies, waits for them, and re-layouts  54.1 us (5%)
  between operations  14.1 us (1%)
    psum x4, waiting for transfers between devices, spread(): return lax.psum(kept, axis)  344 us
    psum x4, blocking collectives, spread(): return lax.psum(kept, axis)  261 us
    all_gather x1, waiting for transfers between devices, on_device(): parts = lax.all_gather(contributions, 'grp', axis=0, tiled=True)  55.3 us
    another operation x4, matrix products, factor_panel(): lax.linalg.triangular_solve(chol, below, left_side=False, lower=True, tra...  54.6 us
    another operation x12, other arithmetic, factor_panel(): chol = jnp.linalg.cholesky(block)  49.7 us
    another operation x8, other arithmetic, factor_panel(): lax.linalg.triangular_solve(chol, below, left_side=False, lower=True, tra...  41.8 us
    select_n x8, other arithmetic, spread(): jnp.where(lax.axis_index(axis) == source, value, 0).astype(value.dtype)  36.3 us
    unnamed x13, local copies, waits for them, and re-layouts  29.1 us
  transfers between devices with their start and end apart: 5, of which 5 were waited for; matrix products, arithmetic and copies ran while one was open for 1% of the time, Pallas kernels for 0%

commit v1 on v0

v1 whole, which is shorter than its diff:
```python
import functools

import jax
import jax.numpy as jnp
from jax import lax
from jax.experimental import pallas as pl
from jax.experimental.pallas import tpu as pltpu
from jax.sharding import PartitionSpec as P

PANELS = 4
W = 128
LEAD = PANELS * W
PACK = 16
F32 = jnp.float32
BF16 = jnp.bfloat16


def ldl_inverse(m_ref, d_ref):
    lane = lax.broadcasted_iota(jnp.int32, (8, W), 1)
    sub = lax.broadcasted_iota(jnp.int32, (8, W), 0)
    for g in range(W // 8):
        c0 = 8 * g
        rest = W - c0 - 8
        top = m_ref[c0 : c0 + 8, :]
        ctop = [jnp.broadcast_to(top[:, c0 + j : c0 + j + 1], (8, W)) for j in range(8)]
        if rest:
            low = m_ref[c0 + 8 :, :]
            clow = [jnp.broadcast_to(low[:, c0 + j : c0 + j + 1], (rest, W)) for j in range(8)]
        inside = (lane >= c0) & (lane < c0 + 8)
        rows = jnp.where(inside, (lane == sub + c0).astype(F32), top)
        dvec = jnp.zeros((8, W), F32)
        llow = []
        for j in range(8):
            piv = ctop[j][j : j + 1, :]
            rec = 1.0 / piv
            dvec = jnp.where(sub == j, piv, dvec)
            lt = jnp.where(sub > j, ctop[j] * rec, 0.0)
            ups = [ctop[jj][j : j + 1, :] for jj in range(j + 1, 8)]
            for jj, up in zip(range(j + 1, 8), ups):
                ctop[jj] = ctop[jj] - lt * up
            rows = rows - lt * rows[j : j + 1, :]
            if rest:
                ll = clow[j] * rec
                for jj, up in zip(range(j + 1, 8), ups):
                    clow[jj] = clow[jj] - ll * up
                llow.append(ll)
        m_ref[c0 : c0 + 8, :] = rows
        d_ref[c0 : c0 + 8, :] = dvec
        if rest:
            lanes = lax.broadcasted_iota(jnp.int32, (rest, W), 1)
            acc = jnp.where((lanes >= c0) & (lanes < c0 + 8), 0.0, low)
            for j in range(8):
                acc = acc - llow[j] * rows[j : j + 1, :]
            m_ref[c0 + 8 :, :] = acc


def factor_kernel(me_ref, lead_ref, own_ref, l_ref, w_ref, t_ref, m_ref, d_ref):
    me = me_ref[0]
    row = lax.broadcasted_iota(jnp.int32, (W, W), 0)
    col = lax.broadcasted_iota(jnp.int32, (W, W), 1)
    t_ref[:, :LEAD] = lead_ref[...]
    t_ref[:, LEAD:] = own_ref[...]

    def step(k, carry):
        here = pl.ds(pl.multiple_of(k * W, W), W)
        diag = t_ref[here, here]
        diag = 0.5 * (diag + diag.T)
        m_ref[...] = diag
        ldl_inverse(m_ref, d_ref)
        d = d_ref[...]
        minv = jnp.where(col <= row, m_ref[...], 0.0) / d
        piv = d.astype(BF16).astype(F32)
        t = t_ref[here, :]
        own = jnp.where(me == k, diag, t[:, LEAD:])
        q = jnp.dot(
            minv,
            jnp.concatenate([t[:, :LEAD], own], axis=1),
            precision=lax.Precision.HIGHEST,
            preferred_element_type=F32,
        )
        q_own = q[:, LEAD:]
        q_own = jnp.where((me > k) | ((me == k) & (col >= row)), q_own, 0.0)
        q_own = q_own.astype(BF16).astype(F32)
        q_lead = q[:, :LEAD].astype(BF16)
        pw = jnp.concatenate([piv] * PANELS, axis=1)
        coef = (q_lead.astype(F32) * pw).astype(BF16).astype(F32).T.astype(BF16)
        t_ref[...] = t_ref[...] - jnp.dot(
            coef,
            jnp.concatenate([q_lead, q_own.astype(BF16)], axis=1),
            preferred_element_type=F32,
        )
        l_ref[:, here] = q_own.T.astype(BF16)
        w_ref[here, :] = (q_own * piv).astype(BF16)
        return carry

    lax.fori_loop(0, PANELS, step, 0)


def factor(me, lead, own):
    return pl.pallas_call(
        factor_kernel,
        out_shape=(
            jax.ShapeDtypeStruct((W, LEAD), BF16),
            jax.ShapeDtypeStruct((LEAD, W), BF16),
        ),
        in_specs=[
            pl.BlockSpec(memory_space=pltpu.SMEM),
            pl.BlockSpec(memory_space=pltpu.VMEM),
            pl.BlockSpec(memory_space=pltpu.VMEM),
        ],
        out_specs=(pl.BlockSpec(memory_space=pltpu.VMEM), pl.BlockSpec(memory_space=pltpu.VMEM)),
        scratch_shapes=[
            pltpu.VMEM((LEAD, LEAD + W), F32),
            pltpu.VMEM((W, W), F32),
            pltpu.VMEM((W, W), F32),
        ],
        name="factor",
    )(me, lead, own)


CHUNK = 1024


def update_kernel(me_ref, maps_ref, front_ref, l_ref, w_ref, parts_ref, flag_ref, out_ref, list_ref):
    s = pl.program_id(0)
    me = me_ref[0]
    groups = maps_ref.shape[0]

    @pl.when(s == 0)
    def _():
        count = jnp.int32(0)
        for g in range(groups):
            mine = maps_ref[g, lax.rem(me, 8)] == me
            list_ref[count] = g
            count = count + mine.astype(jnp.int32)
        list_ref[groups] = count

    @pl.when(me < PANELS)
    def _():
        out_ref[...] = l_ref[:, pl.ds(pl.multiple_of(jnp.minimum(me, PANELS - 1) * W, W), W)].astype(F32)

    @pl.when(me >= PANELS)
    def _():
        out_ref[...] = front_ref[...] - jnp.dot(l_ref[...], w_ref[...], preferred_element_type=F32)

        def add(n, carry):
            g = list_ref[n]
            for i in range(CHUNK // W):

                @pl.when(maps_ref[g, i] == s * (CHUNK // W) + i)
                def _():
                    out_ref[i * W : (i + 1) * W, :] += parts_ref[g, i * W : (i + 1) * W, :].astype(F32)

            return carry

        lax.fori_loop(0, list_ref[groups], add, 0)

        @pl.when(lax.div(me, CHUNK // W) == s)
        def _():
            at = pl.ds(pl.multiple_of(lax.rem(me, CHUNK // W) * W, W), W)
            row = lax.broadcasted_iota(jnp.int32, (W, W), 0)
            col = lax.broadcasted_iota(jnp.int32, (W, W), 1)
            out_ref[at, :] += jnp.where(row == col, flag_ref[...].astype(F32), 0.0)

        @pl.when(s == 0)
        def _():
            out_ref[:LEAD, :] = jnp.zeros((LEAD, W), F32)


def update(me, maps, front, all_l, w, parts, flags):
    order = front.shape[0]
    groups = parts.shape[0]
    return pl.pallas_call(
        update_kernel,
        out_shape=jax.ShapeDtypeStruct((order, W), F32),
        grid=(order // CHUNK,),
        in_specs=[
            pl.BlockSpec(memory_space=pltpu.SMEM),
            pl.BlockSpec(memory_space=pltpu.SMEM),
            pl.BlockSpec((CHUNK, W), lambda s: (s, 0)),
            pl.BlockSpec((CHUNK, LEAD), lambda s: (s, 0)),
            pl.BlockSpec((LEAD, W), lambda s: (0, 0)),
            pl.BlockSpec(parts.shape, lambda s: (0, 0, 0)),
            pl.BlockSpec((1, W), lambda s: (0, 0)),
        ],
        out_specs=pl.BlockSpec((CHUNK, W), lambda s: (s, 0)),
        scratch_shapes=[pltpu.SMEM((groups + 1,), jnp.int32)],
        name="update",
    )(me, maps, front, all_l, w, parts, flags)


def on_device(front, contributions, block_map, pivot_flags):
    both = ("grp", "col")
    me = lax.axis_index(both)
    flags = pivot_flags.reshape(1, W)
    child = contributions.shape[1]
    packed = jnp.concatenate(
        [
            contributions[0].astype(BF16),
            jnp.pad(block_map.astype(BF16), ((0, PACK - 1), (0, W - block_map.shape[1]))),
        ],
        axis=0,
    )
    got = lax.all_gather(packed, "grp", axis=0)
    parts = got[:, :child]
    maps = got[:, child, : block_map.shape[1]].astype(jnp.int32)
    mine = lax.dynamic_index_in_dim(maps, lax.axis_index("col"), 1, keepdims=False) == me
    hit = maps[:, :PANELS] == jnp.arange(PANELS, dtype=jnp.int32)[None, :]
    weight = (mine[:, None] & hit).astype(F32)
    added = jnp.sum(
        got[:, :LEAD].reshape(-1, PANELS, W, W).astype(F32) * weight[:, :, None, None], axis=0
    ).reshape(LEAD, W)
    at = jnp.arange(LEAD, dtype=jnp.int32)[:, None] == me * W + jnp.arange(W, dtype=jnp.int32)[None, :]
    own = front[:LEAD] + added + jnp.where(at, flags.astype(F32), 0.0)
    lead = jnp.stack([jnp.where(me == k, own, 0.0) for k in range(PANELS)], axis=1).reshape(LEAD, LEAD)
    lead = lax.psum(lead, both)
    which = me.reshape(1)
    own_l, own_w = factor(which, lead, own)
    all_l = lax.all_gather(own_l, both, axis=0, tiled=True)
    return update(which, maps, front, all_l, own_w, parts, flags)


def solution(mesh):
    return jax.shard_map(
        on_device,
        mesh=mesh,
        in_specs=(
            P(None, ("grp", "col")),
            P("grp", None, "col"),
            P("grp", None),
            P(("grp", "col")),
        ),
        out_specs=P(None, ("grp", "col")),
        check_vma=False,
    )
```

time: 1040 us -> 349 us (0.34); the launches traced: 1020 us -> 346 us
  blocking collectives: 277 us -> 0 us
  other arithmetic: 184 us -> 8.63 us
  waiting for transfers between devices: 400 us -> 276 us
  matrix products: 94.5 us -> 0 us
  local copies, waits for them, and re-layouts: 54.1 us -> 6.46 us
  Pallas kernels: 0 us -> 41.4 us
    psum x4 -> x0, blocking collectives: 261 us -> none  [spread(): return lax.psum(kept, axis)]
    psum x4 -> x1, waiting for transfers between devices: 344 us -> 148 us  [on_device(): lead = lax.psum(lead, both)]
    another operation x25 -> x3, other arithmetic: 91.9 us -> 1.14 us  [on_device(): jnp.stack([jnp.where(me == k, own, 0.0) for k in range(PANELS)], axis=1)]
    all_gather x1 -> x2, waiting for transfers between devices: 55.3 us -> 129 us  [the longest x1 75.3 us: on_device(): all_l = lax.all_gather(own_l, both, axis=0, tiled=True)]
    another operation x4 -> x0, matrix products: 54.6 us -> none  [factor_panel(): lax.linalg.triangular_solve(chol, below, left_side=False, lower=True, tra...]
    scatter-add x2 -> x0, other arithmetic: 44.3 us -> none  [the longest x1 26.4 us: on_device(): tiles = front.reshape(blocks, width, width).at[maps.reshape(-1)].add(chosen)]
    pallas_call x0 -> x2, Pallas kernels: none -> 41.4 us  [the longest x1 21 us: factor(): pl.pallas_call(factor_kernel, out_shape=(jax.ShapeDtypeStruct((W, LEAD),...]
    dot_general x4 -> x0, matrix products: 39.9 us -> none  [the longest x3 25.6 us: factor_panel(): lax.dot_general(earlier, coef, (((1,), (1,)), ((), ())), preferred_elemen...]
  transfers between devices with their start and end apart: 5 -> 3, of which waited for: 5 -> 3; matrix products, arithmetic and copies ran while one was open for 1% -> 2% of each run, Pallas kernels for 0% -> 0%
where the time goes in v1:
time: 349 us; the launch traced here: 346 us
  waiting for transfers between devices  276 us (79%)
  Pallas kernels  41.4 us (12%)
  between operations  13.2 us (4%)
  other arithmetic  8.63 us (2%)
  local copies, waits for them, and re-layouts  6.46 us (2%)
    psum x1, waiting for transfers between devices, on_device(): lead = lax.psum(lead, both)  148 us
    all_gather x1, waiting for transfers between devices, on_device(): all_l = lax.all_gather(own_l, both, axis=0, tiled=True)  75.3 us
    all_gather x1, waiting for transfers between devices, on_device(): got = lax.all_gather(packed, 'grp', axis=0)  53.5 us
    pallas_call x1, Pallas kernels, factor(): pl.pallas_call(factor_kernel, out_shape=(jax.ShapeDtypeStruct((W, LEAD),...  21 us
    pallas_call x1, Pallas kernels, update(): pl.pallas_call(update_kernel, out_shape=jax.ShapeDtypeStruct((order, W),...  20.4 us
  transfers between devices with their start and end apart: 3, of which 3 were waited for; matrix products, arithmetic and copies ran while one was open for 2% of the time, Pallas kernels for 0%

profile of v1, /device:TPU:9, one launch (start us, length us, event | category | flops | bytes accessed | tf_op | source)
XLA Modules:
  0.0 346.1 jit_solution(9906142855093660753)
XLA Ops:
  6.5 0.7 convert_element_type.29
  7.2 1.1 convert_bitcast_fusion
  8.3 0.7 fusion.1
  9.0 0.0 all-reduce.3.cloned.1.call-start
  9.1 0.7 convert_element_type.34
  9.7 53.5 %all-gather.6.cloned.1.call-done = bf16[16640,128]{1,0:T(8,128)(2,1)} async-done(((bf16[1040,128]{1,0:T(8,128)(2,1)}), bf16[16640,128]{1,0:T(8,128)(2,1)}) %all-gather.6.cloned.1.call-update) | async-done | bytes 4259856 | tf_op jit(solution)/shard_map/all_gather | solution.py:204
  63.2 0.8 slice_convert_fusion
  64.0 0.1 copy.8
  64.0 0.4 compare_reduce_fusion
  64.5 0.1 copy.9
  64.6 0.1 mul.20
  64.7 3.2 multiply_reduce_fusion
  67.9 1.0 select_bitcast_fusion.3
  68.9 0.1 select_bitcast_fusion.2
  68.9 0.1 pad_maximum_fusion
  69.0 0.3 copy.10
  69.4 1.3 copy.11
  70.7 0.0 all-gather.4.cloned.1.call-start
  70.8 147.6 %all-reduce.3.cloned.1.call-done.lead_ref = f32[512,512]{1,0:T(8,128)} async-done(((f32[512,512]{1,0:T(8,128)}), f32[512,512]{1,0:T(8,128)}) %all-reduce.3.cloned.1.call-update) | async-done | bytes 1048592 | tf_op jit(solution)/shard_map/psum | solution.py:216
  218.3 21.0 %factor.1 = (bf16[128,512]{1,0:T(8,128)(2,1)}, bf16[512,128]{1,0:T(8,128)(2,1)}) custom-call(s32[1]{0:T(128)} %bitcast.me_ref, f32[512,512]{1,0:T(8,128)} %all-reduce.3.cloned.1.call-done.lead_ref, f32[512,128]{1,0:T(8,128)} %copy-done), custom_call_target="tpu_custom_call" | custom-call | tf_op jit(solution)/shard_map/factor/pallas_call | solution.py:100
  239.3 0.0 all-gather.4.cloned.1.call-update
  239.4 4.6 %slice.22.parts_ref = bf16[16,1024,128]{2,1,0:T(8,128)(2,1)} slice(bf16[16,1040,128]{2,1,0:T(8,128)(2,1)} %bitcast.24), slice={[0:16], [0:1024], [0:128]} | slice | bytes 8388608 | tf_op jit(solution)/shard_map/slice | solution.py:205
  243.9 75.3 %all-gather.4.cloned.1.call-done.l_ref = bf16[16384,512]{1,0:T(8,128)(2,1)} async-done(((bf16[128,512]{1,0:T(8,128)(2,1)}), bf16[16384,512]{1,0:T(8,128)(2,1)}) %all-gather.4.cloned.1.call-update) | async-done | bytes 16777232 | tf_op jit(solution)/shard_map/all_gather | solution.py:219
  319.2 20.4 %update.1 = f32[16384,128]{1,0:T(8,128)} custom-call(s32[1]{0:T(128)} %bitcast.me_ref, s32[16,8]{1,0:T(8,128)} %bitcast.27, f32[16384,128]{1,0:T(8,128)} %front_ref.1, bf16[16384,512]{1,0:T(8,128)(2,1)} %all-gather.4.cloned.1.call-done.l_ref, bf16[512,128]{1,0:T(8,128)(2,1)} %get-tuple-element.8.w_ref, bf16[16,1024,128]{2,1,0:T(8,128)(2,1)} %slice.22.parts_ref, ...), custom_call_target="tpu_custom_call" | custom-call | tf_op jit(solution)/shard_map/update/pallas_call | solution.py:173
  (10 shorter events, 0.1 us)
Async XLA Ops:
  6.5 56.7 %all-gather.6.cloned.1.call-start = ((), (), s32[]{:S(2)}) async-start(), calls=%async_computation.2 | async-start | bytes 4526080 | tf_op jit(solution)/shard_map/all_gather | solution.py:204
  9.0 209.3 %all-reduce.3.cloned.1.call-start = ((), (), s32[]{:S(2)}) async-start(), calls=%async_computation | async-start | bytes 2097152 | tf_op jit(solution)/shard_map/psum | solution.py:216
  64.0 5.4 %copy-start.1 = (s32[16,1,8]{2,1,0:T(1,128)}, s32[16,1,8]{2,1,0:T(1,128)S(1)}, u32[]{:S(2)}) copy-start(s32[16,1,8]{2,1,0:T(1,128)S(1)} %slice_convert_fusion) | copy-start | bytes 1540
  68.9 149.4 %copy-start = (f32[512,128]{1,0:T(8,128)}, f32[512,128]{1,0:T(8,128)S(1)}, u32[]{:S(2)}) copy-start(f32[512,128]{1,0:T(8,128)S(1)} %get-tuple-element.10.own_ref) | copy-start | bytes 786436
  70.7 248.5 %all-gather.4.cloned.1.call-start = ((), (), s32[]{:S(2)}) async-start(), calls=%async_computation.1 | async-start | bytes 16908288 | tf_op jit(solution)/shard_map/all_gather | solution.py:219
Sparse Core Ops, SparseCore 0:
  9.5 53.6 all-gather.5
  70.8 147.4 all-reduce.2
  239.5 79.7 all-gather.3

commit v2 on v1

--- a/solution.py
+++ b/solution.py
@@ -11,6 +11,8 @@
 W = 128
 LEAD = PANELS * W
 PACK = 16
+MESH = pl.DeviceIdType.MESH
+FULL = pl.ds(0, 4)
 F32 = jnp.float32
 BF16 = jnp.bfloat16
 
@@ -54,11 +56,316 @@
             m_ref[c0 + 8 :, :] = acc
 
 
+class Place:
+    def __init__(self):
+        self.g = lax.axis_index("grp")
+        self.c = lax.axis_index("col")
+        self.at = {"x": lax.rem(self.g, 4), "y": lax.div(self.g, 4), "z": lax.div(self.c, 2)}
+        self.core = lax.rem(self.c, 2)
+        self.partner = (self.g, self.at["z"] * 2 + 1 - self.core)
+
+    def near(self, dim, delta):
+        to = dict(self.at)
+        to[dim] = lax.rem(self.at[dim] + delta + 4, 4)
+        return (to["y"] * 4 + to["x"], to["z"] * 2 + self.core)
+
+    def greet(self):
+        barrier = pltpu.get_barrier_semaphore()
+        peers = [self.near(d, s) for d in "xyz" for s in (1, -1)] + [self.partner]
+        for peer in peers:
+            pl.semaphore_signal(barrier, inc=1, device_id=peer, device_id_type=MESH)
+        pl.semaphore_wait(barrier, len(peers))
+
+
+class Wires:
+    def __init__(self, send, recv, count):
+        self.send, self.recv, self.count, self.used = send, recv, count, 0
+
+    def copy(self, ref, device):
+        n = self.used
+        self.used += 1
+        assert n < self.count
+        return pltpu.make_async_remote_copy(
+            src_ref=ref,
+            dst_ref=ref,
+            send_sem=self.send.at[n],
+            recv_sem=self.recv.at[n],
+            device_id=device,
+            device_id_type=MESH,
+        )
+
+
+def gather_stream(place, wires, view, order, rows, middle, across):
+    lo, hi = pl.ds(rows[0], middle - rows[0]), pl.ds(middle, rows[1] - middle)
+    every = pl.ds(rows[0], rows[1] - rows[0])
+    sent = []
+    d2d = []
+
+    def launch(copy, to=None):
+        copy.start()
+        sent.append(copy)
+        if to is not None:
+            to.append(copy)
+        return copy
+
+    for phase, dim in enumerate(order):
+        last = across and phase == len(order) - 1
+
+        def unit(v, r, dim=dim, phase=phase):
+            where = {d: (FULL if d in order[:phase] else place.at[d]) for d in order}
+            where[dim] = v
+            return view(where, r)
+
+        mine = place.at[dim]
+        before, after, far = (lax.rem(mine + n, 4) for n in (3, 1, 2))
+        right, left = place.near(dim, 1), place.near(dim, -1)
+        to_right = launch(wires.copy(unit(mine, every), right))
+        to_left = launch(wires.copy(unit(mine, every), left))
+        if last:
+            launch(wires.copy(unit(mine, every), place.partner), d2d)
+        yield
+        to_right.wait_recv()
+        on_right = launch(wires.copy(unit(before, lo), right))
+        if last:
+            launch(wires.copy(unit(before, every), place.partner), d2d)
+        to_left.wait_recv()
+        on_left = launch(wires.copy(unit(after, hi), left))
+        if last:
+            launch(wires.copy(unit(after, every), place.partner), d2d)
+        yield
+        on_right.wait_recv()
+        on_left.wait_recv()
+        if last:
+            launch(wires.copy(unit(far, every), place.partner), d2d)
+    yield
+    for copy in d2d:
+        copy.wait_recv()
+    for copy in sent:
+        copy.wait_send()
+
+
+def ring_bcast(on, r, wires, whole, lo, hi, right, left, partner=None, other=None):
+    to_right, to_left = wires.copy(whole, right), wires.copy(whole, left)
+    on_right, on_left = wires.copy(lo, right), wires.copy(hi, left)
+    across = wires.copy(whole, partner) if partner is not None else None
+
+    @pl.when(on & (r == 0))
+    def _():
+        to_right.start()
+        to_left.start()
+        if across is not None:
+            across.start()
+
+    yield
+
+    @pl.when(on & (r == 1))
+    def _():
+        to_right.wait_recv()
+        on_right.start()
+        if across is not None:
+            across.start()
+
+    @pl.when(on & (r == 3))
+    def _():
+        to_left.wait_recv()
+        on_left.start()
+        if across is not None:
+            across.start()
+
+    yield
+
+    @pl.when(on & (r == 2))
+    def _():
+        on_right.wait_recv()
+        on_left.wait_recv()
+        if across is not None:
+            across.start()
+
+    yield "got"
+    if across is not None:
+
+        @pl.when(other)
+        def _():
+            across.wait_recv()
+
+        @pl.when(on)
+        def _():
+            across.wait_send()
+
+    @pl.when(on & (r == 0))
+    def _():
+        to_right.wait_send()
+        to_left.wait_send()
+
+    @pl.when(on & (r == 1))
+    def _():
+        on_right.wait_send()
+
+    @pl.when(on & (r == 3))
+    def _():
+        on_left.wait_send()
+
+
+def run(*streams):
+    streams = list(streams)
+    while streams:
+        streams = [s for s in streams if next(s, "end") != "end"]
+
+
+ROWS_A = ((0, 144, 80, "xy"), (144, 272, 208, "yx"), (272, 400, 336, "xy"), (400, 528, 464, "yx"))
+ROWS_B = ((528, 656, 592, "xy"), (656, 784, 720, "yx"), (784, 912, 848, "xy"), (912, 1040, 976, "yx"))
+WIRES_1 = 146
+
+
+def exchange_kernel(packed_ref, own_ref, cg_ref, b_ref, lead_ref, flead_ref, load_sem, send_sem, recv_sem):
+    place = Place()
+    wires = Wires(send_sem, recv_sem, WIRES_1)
+    x, y, z = place.at["x"], place.at["y"], place.at["z"]
+    me = place.g * 8 + place.c
+    load = pltpu.make_async_copy(packed_ref, cg_ref.at[y, x], load_sem.at[0])
+    load.start()
+    load_lead = pltpu.make_async_copy(own_ref, flead_ref, load_sem.at[1])
+    load_own = pltpu.make_async_copy(own_ref, b_ref, load_sem.at[2])
+    load_own.start()
+
+    @pl.when(place.g == 0)
+    def _():
+        load_lead.start()
+        load_lead.wait()
+
+    load.wait()
+    load_own.wait()
+    place.greet()
+
+    def view(where, rows):
+        return cg_ref.at[where["y"], where["x"], rows, :]
+
+    def spread(j):
+        first, second = ("x", "y") if j % 2 == 0 else ("y", "x")
+        base = j * W
+        refs = [flead_ref.at[pl.ds(base, W)], flead_ref.at[pl.ds(base, W // 2)], flead_ref.at[pl.ds(base + W // 2, W // 2)]]
+        low = place.c < PANELS
+        for dim, on in ((first, low & (place.at[second] == 0)), (second, low)):
+            yield from ring_bcast(on, place.at[dim], wires, *refs, place.near(dim, 1), place.near(dim, -1))
+
+    def streams(table):
+        return [gather_stream(place, wires, view, order, (r0, r1), mid, False) for r0, r1, mid, order in table]
+
+    run(*streams(ROWS_A), *[spread(j) for j in range(PANELS)])
+    rest = streams(ROWS_B)
+    for s in rest:
+        next(s)
+
+    pick = lax.broadcasted_iota(jnp.int32, (PACK, W), 0)
+    weights = []
+    for g in range(16):
+        entry = cg_ref[g // 4, g % 4, 0:PACK, :].astype(F32)
+        target = jnp.sum(jnp.where(pick == place.c, entry, 0.0), axis=0, keepdims=True)
+        own_hit = target == me.astype(F32)
+        lead_hit = target == place.c.astype(F32)
+        here = [entry[k : k + 1, :] == float(k) for k in range(PANELS)]
+        weights.append(
+            (
+                [jnp.where(own_hit & h, 1.0, 0.0) for h in here],
+                [jnp.where(lead_hit & h, 1.0, 0.0) for h in here],
+            )
+        )
+    for k in range(PANELS):
+        at = pl.ds(k * W, W)
+        acc_own, acc_lead = b_ref[at, :], flead_ref[at, :]
+        for g in range(16):
+            block = cg_ref[g // 4, g % 4, PACK + k * W : PACK + (k + 1) * W, :].astype(F32)
+            acc_own = acc_own + block * weights[g][0][k]
+            acc_lead = acc_lead + block * weights[g][1][k]
+        b_ref[at, :] = acc_own
+        for l in range(k, PANELS):
+
+            @pl.when(place.c == l)
+            def _():
+                lead_ref[l, k] = acc_lead
+
+    def lead_unit(l, k):
+        on = place.core == l % 2
+        r = lax.rem(z - l // 2 + 4, 4)
+        refs = [lead_ref.at[l, k], lead_ref.at[l, k, pl.ds(0, W // 2)], lead_ref.at[l, k, pl.ds(W // 2, W // 2)]]
+        return ring_bcast(
+            on, r, wires, *refs, place.near("z", 1), place.near("z", -1), place.partner, place.core != l % 2
+        )
+
+    run(*[lead_unit(l, k) for k in range(PANELS) for l in range(k, PANELS)], *rest)
+
+
+def exchange(packed, own):
+    rows = packed.shape[0]
+    vmem = pl.BlockSpec(memory_space=pltpu.VMEM)
+    return pl.pallas_call(
+        exchange_kernel,
+        out_shape=(
+            jax.ShapeDtypeStruct((4, 4, rows, W), BF16),
+            jax.ShapeDtypeStruct((LEAD, W), F32),
+            jax.ShapeDtypeStruct((PANELS, PANELS, W, W), F32),
+        ),
+        in_specs=[pl.BlockSpec(memory_space=pl.ANY)] * 2,
+        out_specs=(vmem, vmem, vmem),
+        scratch_shapes=[
+            pltpu.VMEM((LEAD, W), F32),
+            pltpu.SemaphoreType.DMA((3,)),
+            pltpu.SemaphoreType.DMA((WIRES_1,)),
+            pltpu.SemaphoreType.DMA((WIRES_1,)),
+        ],
+        compiler_params=pltpu.CompilerParams(collective_id=0, has_side_effects=True),
+        name="exchange",
+    )(packed, own)
+
+
+TILES = (((0, 48), (48, 96), (96, 128)), ((0, 48), (48, 80), (80, 128)), ((0, 32), (32, 80), (80, 128)), ((0, 48), (48, 96), (96, 128)))
+ORDERS = ("xyz", "yzx", "zxy")
+WIRES_3 = 192
+
+
+def gather_kernel(l_ref, all_ref, load_sem, send_sem, recv_sem):
+    place = Place()
+    wires = Wires(send_sem, recv_sem, WIRES_3)
+    own = all_ref.at[:, place.at["y"], place.at["x"], place.at["z"], place.core]
+    load = pltpu.make_async_copy(l_ref, own, load_sem.at[0])
+    load.start()
+    load.wait()
+    place.greet()
+
+    def stream(k, p):
+        def view(where, rows):
+            return all_ref.at[k, where["y"], where["x"], where["z"], place.core, rows, :]
+
+        r0, r1 = TILES[k][p]
+        half = (r1 - r0) // 32 * 16 if (k + p) % 2 else (r1 - r0 + 16) // 32 * 16
+        return gather_stream(place, wires, view, ORDERS[p], (r0, r1), r0 + half, True)
+
+    run(*[stream(k, p) for k in range(PANELS) for p in range(3)])
+
+
+def gather(own_l):
+    return pl.pallas_call(
+        gather_kernel,
+        out_shape=jax.ShapeDtypeStruct((PANELS, 4, 4, 4, 2, W, W), BF16),
+        in_specs=[pl.BlockSpec(memory_space=pl.ANY)],
+        out_specs=pl.BlockSpec(memory_space=pltpu.VMEM),
+        scratch_shapes=[
+            pltpu.SemaphoreType.DMA((1,)),
+            pltpu.SemaphoreType.DMA((WIRES_3,)),
+            pltpu.SemaphoreType.DMA((WIRES_3,)),
+        ],
+        compiler_params=pltpu.CompilerParams(collective_id=1, has_side_effects=True),
+        name="gather",
+    )(own_l)
+
+
 def factor_kernel(me_ref, lead_ref, own_ref, l_ref, w_ref, t_ref, m_ref, d_ref):
     me = me_ref[0]
     row = lax.broadcasted_iota(jnp.int32, (W, W), 0)
     col = lax.broadcasted_iota(jnp.int32, (W, W), 1)
-    t_ref[:, :LEAD] = lead_ref[...]
+    for k in range(PANELS):
+        for l in range(PANELS):
+            t_ref[k * W : (k + 1) * W, l * W : (l + 1) * W] = lead_ref[l, k] if l >= k else jnp.zeros((W, W), F32)
     t_ref[:, LEAD:] = own_ref[...]
 
     def step(k, carry):
@@ -89,7 +396,7 @@
             jnp.concatenate([q_lead, q_own.astype(BF16)], axis=1),
             preferred_element_type=F32,
         )
-        l_ref[:, here] = q_own.T.astype(BF16)
+        l_ref[k] = q_own.T.astype(BF16)
         w_ref[here, :] = (q_own * piv).astype(BF16)
         return carry
 
@@ -100,7 +407,7 @@
     return pl.pallas_call(
         factor_kernel,
         out_shape=(
-            jax.ShapeDtypeStruct((W, LEAD), BF16),
+            jax.ShapeDtypeStruct((PANELS, W, W), BF16),
             jax.ShapeDtypeStruct((LEAD, W), BF16),
         ),
         in_specs=[
@@ -118,13 +425,17 @@
     )(me, lead, own)
 
 
-CHUNK = 1024
-
-
-def update_kernel(me_ref, maps_ref, front_ref, l_ref, w_ref, parts_ref, flag_ref, out_ref, list_ref):
+CHUNK = 2048
+SPAN = CHUNK // W
+
+
+def update_kernel(me_ref, maps_ref, front_ref, l_ref, w_ref, parts_ref, flag_ref, out_ref, list_ref, held, sems):
     s = pl.program_id(0)
     me = me_ref[0]
     groups = maps_ref.shape[0]
+
+    def load(g):
+        return pltpu.make_async_copy(parts_ref.at[g], held.at[g], sems.at[g])
 
     @pl.when(s == 0)
     def _():
@@ -133,31 +444,45 @@
             mine = maps_ref[g, lax.rem(me, 8)] == me
             list_ref[count] = g
             count = count + mine.astype(jnp.int32)
+
+            @pl.when(mine)
+            def _():
+                load(g).start()
+
         list_ref[groups] = count
 
+        for g in range(groups):
+
+            @pl.when(maps_ref[g, lax.rem(me, 8)] == me)
+            def _():
+                load(g).wait()
+
     @pl.when(me < PANELS)
     def _():
-        out_ref[...] = l_ref[:, pl.ds(pl.multiple_of(jnp.minimum(me, PANELS - 1) * W, W), W)].astype(F32)
+        out_ref[...] = l_ref[jnp.minimum(me, PANELS - 1)].astype(F32)
 
     @pl.when(me >= PANELS)
     def _():
-        out_ref[...] = front_ref[...] - jnp.dot(l_ref[...], w_ref[...], preferred_element_type=F32)
+        rows = jnp.concatenate([l_ref[k] for k in range(PANELS)], axis=1)
+        out_ref[...] = front_ref[...] - jnp.dot(rows, w_ref[...], preferred_element_type=F32)
 
         def add(n, carry):
             g = list_ref[n]
-            for i in range(CHUNK // W):
-
-                @pl.when(maps_ref[g, i] == s * (CHUNK // W) + i)
+            for i in range(8):
+                block = maps_ref[g, i] - s * SPAN
+
+                @pl.when((block >= 0) & (block < SPAN))
                 def _():
-                    out_ref[i * W : (i + 1) * W, :] += parts_ref[g, i * W : (i + 1) * W, :].astype(F32)
+                    at = pl.ds(pl.multiple_of(block * W, W), W)
+                    out_ref[at, :] += held[g, PACK + i * W : PACK + (i + 1) * W, :].astype(F32)
 
             return carry
 
         lax.fori_loop(0, list_ref[groups], add, 0)
 
-        @pl.when(lax.div(me, CHUNK // W) == s)
+        @pl.when(lax.div(me, SPAN) == s)
         def _():
-            at = pl.ds(pl.multiple_of(lax.rem(me, CHUNK // W) * W, W), W)
+            at = pl.ds(pl.multiple_of(lax.rem(me, SPAN) * W, W), W)
             row = lax.broadcasted_iota(jnp.int32, (W, W), 0)
             col = lax.broadcasted_iota(jnp.int32, (W, W), 1)
             out_ref[at, :] += jnp.where(row == col, flag_ref[...].astype(F32), 0.0)
@@ -178,45 +503,37 @@
             pl.BlockSpec(memory_space=pltpu.SMEM),
             pl.BlockSpec(memory_space=pltpu.SMEM),
             pl.BlockSpec((CHUNK, W), lambda s: (s, 0)),
-            pl.BlockSpec((CHUNK, LEAD), lambda s: (s, 0)),
+            pl.BlockSpec((PANELS, CHUNK, W), lambda s: (0, s, 0)),
             pl.BlockSpec((LEAD, W), lambda s: (0, 0)),
-            pl.BlockSpec(parts.shape, lambda s: (0, 0, 0)),
+            pl.BlockSpec(memory_space=pl.ANY),
             pl.BlockSpec((1, W), lambda s: (0, 0)),
         ],
         out_specs=pl.BlockSpec((CHUNK, W), lambda s: (s, 0)),
-        scratch_shapes=[pltpu.SMEM((groups + 1,), jnp.int32)],
+        scratch_shapes=[
+            pltpu.SMEM((groups + 1,), jnp.int32),
+            pltpu.VMEM(parts.shape, BF16),
+            pltpu.SemaphoreType.DMA((groups,)),
+        ],
         name="update",
     )(me, maps, front, all_l, w, parts, flags)
 
 
 def on_device(front, contributions, block_map, pivot_flags):
-    both = ("grp", "col")
-    me = lax.axis_index(both)
+    me = lax.axis_index(("grp", "col"))
+    which = me.reshape(1)
+    order = front.shape[0]
     flags = pivot_flags.reshape(1, W)
-    child = contributions.shape[1]
+    entries = jnp.broadcast_to(block_map.reshape(-1, 1).astype(BF16), (block_map.shape[1], W))
     packed = jnp.concatenate(
-        [
-            contributions[0].astype(BF16),
-            jnp.pad(block_map.astype(BF16), ((0, PACK - 1), (0, W - block_map.shape[1]))),
-        ],
-        axis=0,
+        [entries, jnp.zeros((PACK - entries.shape[0], W), BF16), contributions[0].astype(BF16)], axis=0
     )
-    got = lax.all_gather(packed, "grp", axis=0)
-    parts = got[:, :child]
-    maps = got[:, child, : block_map.shape[1]].astype(jnp.int32)
-    mine = lax.dynamic_index_in_dim(maps, lax.axis_index("col"), 1, keepdims=False) == me
-    hit = maps[:, :PANELS] == jnp.arange(PANELS, dtype=jnp.int32)[None, :]
-    weight = (mine[:, None] & hit).astype(F32)
-    added = jnp.sum(
-        got[:, :LEAD].reshape(-1, PANELS, W, W).astype(F32) * weight[:, :, None, None], axis=0
-    ).reshape(LEAD, W)
     at = jnp.arange(LEAD, dtype=jnp.int32)[:, None] == me * W + jnp.arange(W, dtype=jnp.int32)[None, :]
-    own = front[:LEAD] + added + jnp.where(at, flags.astype(F32), 0.0)
-    lead = jnp.stack([jnp.where(me == k, own, 0.0) for k in range(PANELS)], axis=1).reshape(LEAD, LEAD)
-    lead = lax.psum(lead, both)
-    which = me.reshape(1)
+    own = front[:LEAD] + jnp.where(at, flags.astype(F32), 0.0)
+    cg, own, lead = exchange(packed, own)
     own_l, own_w = factor(which, lead, own)
-    all_l = lax.all_gather(own_l, both, axis=0, tiled=True)
+    all_l = gather(own_l).reshape(PANELS, order, W)
+    parts = cg.reshape(16, packed.shape[0], W)
+    maps = parts[:, : block_map.shape[1], 0].astype(jnp.int32)
     return update(which, maps, front, all_l, own_w, parts, flags)
 
 

time: 349 us -> 147 us (0.42)
  waiting for transfers between devices: 276 us -> 0 us
  Pallas kernels: 41.4 us -> 140 us
  between operations: 13.2 us -> 0.03 us
  local copies, waits for them, and re-layouts: 6.46 us -> 0.76 us
    psum x1 -> x0, waiting for transfers between devices: 148 us -> none  [on_device(): lead = lax.psum(lead, both)]
    all_gather x2 -> x0, waiting for transfers between devices: 129 us -> none  [the longest x1 75.3 us: on_device(): all_l = lax.all_gather(own_l, both, axis=0, tiled=True)]
    pallas_call x1 -> x3, Pallas kernels: 21 us -> 123 us  [the longest x1 58.4 us: gather(): pl.pallas_call(gather_kernel, out_shape=jax.ShapeDtypeStruct((PANELS, 4,...]
    slice x1 -> x0, local copies, waits for them, and re-layouts: 4.57 us -> none  [on_device(): parts = got[:, :child]]
    pallas_call x1, Pallas kernels: 20.4 us -> 16.7 us  [update(): pl.pallas_call(update_kernel, out_shape=jax.ShapeDtypeStruct((order, W),...]
  transfers between devices with their start and end apart: 3 -> 0, of which waited for: 3 -> 0; matrix products, arithmetic and copies ran while one was open for 2% -> 0% of each run, Pallas kernels for 0% -> 0%
where the time goes in v2:
time: 147 us
  Pallas kernels  140 us (95%)
  other arithmetic  5.85 us (4%)
    pallas_call x1, Pallas kernels, gather(): pl.pallas_call(gather_kernel, out_shape=jax.ShapeDtypeStruct((PANELS, 4,...  58.4 us
    pallas_call x1, Pallas kernels, exchange(): pl.pallas_call(exchange_kernel, out_shape=(jax.ShapeDtypeStruct((4, 4, ro...  43.9 us
    pallas_call x1, Pallas kernels, factor(): pl.pallas_call(factor_kernel, out_shape=(jax.ShapeDtypeStruct((PANELS, W,...  21 us
    pallas_call x1, Pallas kernels, update(): pl.pallas_call(update_kernel, out_shape=jax.ShapeDtypeStruct((order, W),...  16.7 us

profile of v2, /device:TPU:9, one launch (start us, length us, event | category | flops | bytes accessed | tf_op | source)
XLA Modules:
  0.0 146.6 jit_solution(10877611166706014655)
XLA Ops:
  0.0 0.7 convert_bitcast_fusion.1
  0.7 0.7 convert_element_type.30
  1.3 0.1 pad_maximum_fusion.1
  1.4 1.7 %select_add_fusion.own_ref = f32[512,128]{1,0:T(8,128)} fusion(f32[16384,128]{1,0:T(8,128)} %front_ref.1, f32[128]{0:T(128)S(1)} %convert_element_type.30, s32[128]{0:T(128)S(1)} %iota_add_fusion), kind=kLoop, calls=%fused_computation.1 | loop fusion | flops 196608 | bytes 525312 | tf_op jit(solution)/shard_map/add | solution.py:531
  3.1 1.1 convert_bitcast_fusion
  4.2 0.9 pad_maximum_fusion.packed_ref
  5.1 43.9 %exchange.1 = (bf16[4,4,1040,128]{3,2,1,0:T(8,128)(2,1)}, f32[512,128]{1,0:T(8,128)}, f32[4,4,128,128]{3,2,1,0:T(8,128)}) custom-call(bf16[1040,128]{1,0:T(8,128)(2,1)} %pad_maximum_fusion.packed_ref, f32[512,128]{1,0:T(8,128)} %select_add_fusion.own_ref), custom_call_target="tpu_custom_call" | custom-call | tf_op jit(solution)/shard_map/exchange/pallas_call | solution.py:301
  49.0 0.8 slice_convert_fusion
  49.8 0.8 copy.9
  50.5 21.0 %factor.1 = (bf16[4,128,128]{2,1,0:T(8,128)(2,1)}, bf16[512,128]{1,0:T(8,128)(2,1)}) custom-call(s32[1]{0:T(128)} %bitcast.me_ref, f32[4,4,128,128]{3,2,1,0:T(8,128)} %get-tuple-element.11.lead_ref, f32[512,128]{1,0:T(8,128)} %get-tuple-element.12.own_ref), custom_call_target="tpu_custom_call" | custom-call | tf_op jit(solution)/shard_map/factor/pallas_call | solution.py:407
  71.5 58.4 %gather.1 = bf16[4,4,4,4,2,128,128]{6,5,4,3,2,1,0:T(8,128)(2,1)} custom-call(bf16[4,128,128]{2,1,0:T(8,128)(2,1)} %get-tuple-element.13.l_ref), custom_call_target="tpu_custom_call" | custom-call | tf_op jit(solution)/shard_map/gather/pallas_call | solution.py:347
  129.9 16.7 %update.1 = f32[16384,128]{1,0:T(8,128)} custom-call(s32[1]{0:T(128)} %bitcast.me_ref, s32[16,8]{1,0:T(8,128)} %bitcast.13, f32[16384,128]{1,0:T(8,128)} %front_ref.1, bf16[4,16384,128]{2,1,0:T(8,128)(2,1)} %bitcast.10, bf16[512,128]{1,0:T(8,128)(2,1)} %get-tuple-element.14.w_ref, bf16[16,1040,128]{2,1,0:T(8,128)(2,1)} %bitcast.12, s32[1,128]{1,0:T(1,128)} %bitcast.14), custom_call_target="tpu_custom_call" | custom-call | tf_op jit(solution)/shard_map/update/pallas_call | solution.py:498
  (2 shorter events, 0.0 us)

commit v3 on v2

v3 whole, which is shorter than its diff:
```python
import jax
import jax.numpy as jnp
from jax import lax
from jax.experimental import pallas as pl
from jax.experimental.pallas import tpu as pltpu
from jax.sharding import PartitionSpec as P

PANELS = 4
W = 128
LEAD = PANELS * W
PACK = 16
CHILD = 1024
ROWS = PACK + CHILD
MESH = pl.DeviceIdType.MESH
FULL = pl.ds(0, 4)
F32 = jnp.float32
BF16 = jnp.bfloat16


def ldl_inverse(m_ref, d_ref, ticks):
    lane = lax.broadcasted_iota(jnp.int32, (8, W), 1)
    sub = lax.broadcasted_iota(jnp.int32, (8, W), 0)
    for g in range(W // 8):
        c0 = 8 * g
        rest = W - c0 - 8
        top = m_ref[c0 : c0 + 8, :]
        ctop = [jnp.broadcast_to(top[:, c0 + j : c0 + j + 1], (8, W)) for j in range(8)]
        if rest:
            low = m_ref[c0 + 8 :, :]
            clow = [jnp.broadcast_to(low[:, c0 + j : c0 + j + 1], (rest, W)) for j in range(8)]
        inside = (lane >= c0) & (lane < c0 + 8)
        rows = jnp.where(inside, (lane == sub + c0).astype(F32), top)
        dvec = jnp.zeros((8, W), F32)
        llow = []
        for j in range(8):
            piv = ctop[j][j : j + 1, :]
            rec = 1.0 / piv
            dvec = jnp.where(sub == j, piv, dvec)
            lt = jnp.where(sub > j, ctop[j] * rec, 0.0)
            ups = [ctop[jj][j : j + 1, :] for jj in range(j + 1, 8)]
            for jj, up in zip(range(j + 1, 8), ups):
                ctop[jj] = ctop[jj] - lt * up
            rows = rows - lt * rows[j : j + 1, :]
            if rest:
                ll = clow[j] * rec
                for jj, up in zip(range(j + 1, 8), ups):
                    clow[jj] = clow[jj] - ll * up
                llow.append(ll)
        m_ref[c0 : c0 + 8, :] = rows
        d_ref[c0 : c0 + 8, :] = dvec
        if rest:
            lanes = lax.broadcasted_iota(jnp.int32, (rest, W), 1)
            acc = jnp.where((lanes >= c0) & (lanes < c0 + 8), 0.0, low)
            for j in range(8):
                acc = acc - llow[j] * rows[j : j + 1, :]
            m_ref[c0 + 8 :, :] = acc
        for work in ticks.get(g, ()):
            work()


class Place:
    def __init__(self):
        self.g = lax.axis_index("grp")
        self.c = lax.axis_index("col")
        self.at = {"x": lax.rem(self.g, 4), "y": lax.div(self.g, 4), "z": lax.div(self.c, 2)}
        self.core = lax.rem(self.c, 2)
        self.partner = (self.g, self.at["z"] * 2 + 1 - self.core)

    def near(self, dim, delta):
        to = dict(self.at)
        to[dim] = lax.rem(self.at[dim] + delta + 4, 4)
        return (to["y"] * 4 + to["x"], to["z"] * 2 + self.core)

    def greet(self):
        barrier = pltpu.get_barrier_semaphore()
        peers = [self.near(d, s) for d in "xyz" for s in (1, -1)] + [self.partner]
        for peer in peers:
            pl.semaphore_signal(barrier, inc=1, device_id=peer, device_id_type=MESH)
        pl.semaphore_wait(barrier, len(peers))


class Wires:
    def __init__(self, send, recv, count):
        self.send, self.recv, self.count, self.used = send, recv, count, 0

    def copy(self, ref, device):
        n = self.used
        self.used += 1
        assert n < self.count
        return pltpu.make_async_remote_copy(
            src_ref=ref,
            dst_ref=ref,
            send_sem=self.send.at[n],
            recv_sem=self.recv.at[n],
            device_id=device,
            device_id_type=MESH,
        )


def gather_stream(place, wires, view, order, rows, middle, across):
    lo, hi = pl.ds(rows[0], middle - rows[0]), pl.ds(middle, rows[1] - middle)
    every = pl.ds(rows[0], rows[1] - rows[0])
    sent = []
    d2d = []

    def launch(copy, to=None):
        copy.start()
        sent.append(copy)
        if to is not None:
            to.append(copy)
        return copy

    for phase, dim in enumerate(order):
        last = across and phase == len(order) - 1

        def unit(v, r, dim=dim, phase=phase):
            where = {d: (FULL if d in order[:phase] else place.at[d]) for d in order}
            where[dim] = v
            return view(where, r)

        mine = place.at[dim]
        before, after, far = (lax.rem(mine + n, 4) for n in (3, 1, 2))
        right, left = place.near(dim, 1), place.near(dim, -1)
        to_right = launch(wires.copy(unit(mine, every), right))
        to_left = launch(wires.copy(unit(mine, every), left))
        if last:
            launch(wires.copy(unit(mine, every), place.partner), d2d)
        yield
        to_right.wait_recv()
        on_right = launch(wires.copy(unit(before, lo), right))
        if last:
            launch(wires.copy(unit(before, every), place.partner), d2d)
        to_left.wait_recv()
        on_left = launch(wires.copy(unit(after, hi), left))
        if last:
            launch(wires.copy(unit(after, every), place.partner), d2d)
        yield
        on_right.wait_recv()
        on_left.wait_recv()
        if last:
            launch(wires.copy(unit(far, every), place.partner), d2d)
    yield
    for copy in d2d:
        copy.wait_recv()
    yield
    for copy in sent:
        copy.wait_send()


def ring_bcast(on, r, wires, whole, lo, hi, right, left, partner=None, other=None):
    to_right, to_left = wires.copy(whole, right), wires.copy(whole, left)
    on_right, on_left = wires.copy(lo, right), wires.copy(hi, left)
    across = wires.copy(whole, partner) if partner is not None else None

    @pl.when(on & (r == 0))
    def _():
        to_right.start()
        to_left.start()
        if across is not None:
            across.start()

    yield

    @pl.when(on & (r == 1))
    def _():
        to_right.wait_recv()
        on_right.start()
        if across is not None:
            across.start()

    @pl.when(on & (r == 3))
    def _():
        to_left.wait_recv()
        on_left.start()
        if across is not None:
            across.start()

    yield

    @pl.when(on & (r == 2))
    def _():
        on_right.wait_recv()
        on_left.wait_recv()
        if across is not None:
            across.start()

    if across is not None:
        yield

        @pl.when(other)
        def _():
            across.wait_recv()

        yield

        @pl.when(on)
        def _():
            across.wait_send()

    @pl.when(on & (r == 0))
    def _():
        to_right.wait_send()
        to_left.wait_send()

    @pl.when(on & (r == 1))
    def _():
        on_right.wait_send()

    @pl.when(on & (r == 3))
    def _():
        on_left.wait_send()


class Round:
    def __init__(self, streams):
        self.streams = list(streams)

    def __call__(self):
        for s in self.streams:
            next(s, None)


TILES = ((4, 2, 2), (3, 3, 2), (4, 2, 2), (3, 2, 3))
ORDERS = ("xyz", "yzx", "zxy")
WIRES = 5 * 10 + 8 * 8 + 8 * 4 + 8 * 4 + 16 * 12
SLOTS = (2, 5, 8, 11, 14)


def panels_kernel(
    head_ref,
    child_ref,
    map_ref,
    flag_ref,
    all_ref,
    cg_ref,
    w_ref,
    maps_ref,
    own_ref,
    flead_ref,
    lead_ref,
    q_ref,
    coef_ref,
    m_ref,
    d_ref,
    rhs_ref,
    send_sem,
    recv_sem,
):
    place = Place()
    wires = Wires(send_sem, recv_sem, WIRES)
    x, y, z = place.at["x"], place.at["y"], place.at["z"]
    me = place.g * 8 + place.c
    low = place.c < PANELS
    row = lax.broadcasted_iota(jnp.int32, (W, W), 0)
    col = lax.broadcasted_iota(jnp.int32, (W, W), 1)

    entry = lax.broadcasted_iota(jnp.int32, (PACK, W), 0)
    packed = jnp.zeros((PACK, W), F32)
    for i in range(8):
        packed = jnp.where(entry == i, map_ref[0, i].astype(F32), packed)
    cg_ref[y, x, 0:PACK, :] = packed.astype(BF16)
    cg_ref[y, x, PACK:ROWS, :] = child_ref[0].astype(BF16)
    own_ref[...] = head_ref[...]
    for k in range(PANELS):

        @pl.when(me == k)
        def _():
            at = pl.ds(k * W, W)
            own_ref[at, :] += jnp.where(row == col, flag_ref[...].astype(F32), 0.0)

    @pl.when((place.g == 0) & low)
    def _():
        flead_ref[...] = own_ref[...]

    place.greet()

    def child_view(where, rows):
        return cg_ref.at[where["y"], where["x"], rows, :]

    def child_stream(r0, r1, order):
        middle = r0 + (r1 - r0 + 16) // 32 * 16
        return gather_stream(place, wires, child_view, order, (r0, r1), middle, False)

    def spread(j):
        first, second = ("x", "y") if j % 2 == 0 else ("y", "x")
        base = j * W
        half = W // 2
        refs = [flead_ref.at[pl.ds(at, size)] for at, size in ((base, W), (base, half), (base + half, half))]
        for dim, on in ((first, low & (place.at[second] == 0)), (second, low)):
            yield from ring_bcast(on, place.at[dim], wires, *refs, place.near(dim, 1), place.near(dim, -1))

    def lead_unit(l, k):
        on = place.core == l % 2
        r = lax.rem(z - l // 2 + 4, 4)
        half = W // 2
        refs = [lead_ref.at[l, k], lead_ref.at[l, k, pl.ds(0, half)], lead_ref.at[l, k, pl.ds(half, half)]]
        return ring_bcast(
            on, r, wires, *refs, place.near("z", 1), place.near("z", -1), place.partner, place.core != l % 2
        )

    def panel_stream(k, p):
        def view(where, rows):
            return all_ref.at[k, where["y"], where["x"], where["z"], place.core, rows, :]

        r0 = 16 * sum(TILES[k][:p])
        n = TILES[k][p]
        half = (n // 2 if (k + p) % 2 else (n + 1) // 2) * 16
        return gather_stream(place, wires, view, ORDERS[p], (r0, r0 + 16 * n), r0 + half, True)

    def first_row(s):
        return PACK + s * W if s else 0

    a = [
        Round(
            [
                child_stream(first_row(s), PACK + s * W + 64, "xy"),
                child_stream(PACK + s * W + 64, PACK + s * W + W, "yx"),
                spread(s),
            ]
        )
        for s in range(PANELS)
    ]
    far = PACK + LEAD
    b = [
        Round([child_stream(far + n * W, far + (n + 1) * W, "xy" if n % 2 == 0 else "yx") for n in (m, m + 1)])
        for m in (0, 2)
    ]
    lead = [Round([lead_unit(l, k) for l in range(k, PANELS)]) for k in range(PANELS)]
    g = [Round([panel_stream(k, p) for p in range(3)]) for k in range(PANELS)]

    def assemble(k):
        at = pl.ds(k * W, W)
        acc_own, acc_lead = own_ref[at, :], flead_ref[at, :]
        for child in range(16):
            cy, cx = child // 4, child % 4
            names = cg_ref[cy, cx, 0:PACK, :].astype(F32)
            target = jnp.sum(jnp.where(entry == place.c, names, 0.0), axis=0, keepdims=True)
            here = names[k : k + 1, :] == float(k)
            mine = jnp.where((target == me.astype(F32)) & here, 1.0, 0.0)
            first = jnp.where((target == place.c.astype(F32)) & here, 1.0, 0.0)
            block = cg_ref[cy, cx, PACK + k * W : PACK + (k + 1) * W, :].astype(F32)
            acc_own = acc_own + block * mine
            acc_lead = acc_lead + block * first
            if k == 0:
                diagonal = lax.broadcasted_iota(jnp.int32, (PACK, W), 1) == entry
                line = jnp.sum(jnp.where(diagonal, names, 0.0), axis=0, keepdims=True)
                maps_ref[child : child + 1, :] = line.astype(jnp.int32)
        own_ref[at, :] = acc_own
        for l in range(k, PANELS):

            @pl.when(place.c == l)
            def _():
                lead_ref[l, k] = acc_lead

    def panel(k, plan):
        width = PANELS - 1 - k
        at = pl.ds(k * W, W)
        base = jnp.concatenate([lead_ref[l, k] for l in range(k, PANELS)] + [own_ref[at, :]], axis=1)
        if k:
            base = base - jnp.dot(
                coef_ref[k * W : (k + 1) * W, : k * W], q_ref[: k * W, k * W :], preferred_element_type=F32
            )
        diag = base[:, :W]
        diag = 0.5 * (diag + diag.T)
        m_ref[...] = diag
        rhs_ref[:, :W] = jnp.where(me == k, diag, base[:, (width + 1) * W :])
        if width:
            rhs_ref[:, W : W + width * W] = base[:, W : W + width * W]
        ldl_inverse(m_ref, d_ref, dict(zip(SLOTS, plan)))
        d = d_ref[...]
        minv = jnp.where(col <= row, m_ref[...], 0.0) / d
        piv = d.astype(BF16).astype(F32)
        rhs = rhs_ref[:, : W + width * W]
        q = jnp.dot(minv, rhs, precision=lax.Precision.HIGHEST, preferred_element_type=F32)
        own = jnp.where((me > k) | ((me == k) & (col >= row)), q[:, :W], 0.0).astype(BF16).astype(F32)
        all_ref[k, y, x, z, place.core] = own.T.astype(BF16)
        g[k]()
        w_ref[k * W : (k + 1) * W, :] = (own * piv).astype(BF16)
        q_ref[k * W : (k + 1) * W, LEAD:] = own.astype(BF16)
        for i in range(width):
            l = k + 1 + i
            part = q[:, (1 + i) * W : (2 + i) * W].astype(BF16)
            q_ref[k * W : (k + 1) * W, l * W : (l + 1) * W] = part
            coef_ref[l * W : (l + 1) * W, k * W : (k + 1) * W] = (
                (part.astype(F32) * piv).astype(BF16).astype(F32).T.astype(BF16)
            )

    def join(k):
        return lambda: assemble(k)

    for s in range(PANELS):
        a[s]()
    for s in range(PANELS):
        a[s]()
    for work in (a[0], a[0], a[1], a[0], join(0), lead[0], a[1], lead[0], a[2], a[1], lead[0], join(1), lead[0]):
        work()
    lead[1]()
    a[2]()
    panel(
        0,
        (
            (lead[1], a[3]),
            (lead[1], a[2]),
            (lead[1], join(2), lead[2]),
            (a[3], b[0]),
            (lead[2], a[3]),
        ),
    )
    panel(
        1,
        (
            (g[0], lead[2]),
            (join(3), lead[3], lead[2], b[0]),
            (g[0], lead[3]),
            (b[0], g[0]),
            (lead[3],),
        ),
    )
    panel(
        2,
        (
            (g[0], lead[3], g[1]),
            (b[0], g[1]),
            (g[0],),
            (g[1], b[0], b[1]),
            (g[0],),
        ),
    )
    panel(
        3,
        (
            (g[2], g[1], b[1]),
            (g[2], g[0]),
            (g[1], b[1]),
            (g[2],),
            (g[1], b[1]),
        ),
    )
    for work in (g[3], g[2], g[3], g[1], g[3], g[2], b[1], g[3], g[2], g[3], g[2], g[3], g[3]):
        work()
    for group in a + b + lead + g:
        for stream in group.streams:
            for _ in stream:
                pass
    assert wires.used == WIRES


def panels(head, contributions, block_map, flags):
    vmem = pl.BlockSpec(memory_space=pltpu.VMEM)
    return pl.pallas_call(
        panels_kernel,
        out_shape=(
            pltpu.VMEM((PANELS, 4, 4, 4, 2, W, W), BF16),
            pltpu.VMEM((4, 4, ROWS, W), BF16),
            pltpu.VMEM((LEAD, W), BF16),
            jax.ShapeDtypeStruct((16, W), jnp.int32),
        ),
        in_specs=[vmem, vmem, pl.BlockSpec(memory_space=pltpu.SMEM), vmem],
        out_specs=(vmem, vmem, vmem, vmem),
        scratch_shapes=[
            pltpu.VMEM((LEAD, W), F32),
            pltpu.VMEM((LEAD, W), F32),
            pltpu.VMEM((PANELS, PANELS, W, W), F32),
            pltpu.VMEM((LEAD, LEAD + W), BF16),
            pltpu.VMEM((LEAD, LEAD), BF16),
            pltpu.VMEM((W, W), F32),
            pltpu.VMEM((W, W), F32),
            pltpu.VMEM((W, LEAD), F32),
            pltpu.SemaphoreType.DMA((WIRES,)),
            pltpu.SemaphoreType.DMA((WIRES,)),
        ],
        compiler_params=pltpu.CompilerParams(
            collective_id=0, has_side_effects=True, vmem_limit_bytes=VMEM_PANELS
        ),
        name="panels",
    )(head, contributions, block_map, flags)


VMEM_PANELS = 12 * 2**20
VMEM_UPDATE = 12 * 2**20
CHUNK = 2048
SPAN = CHUNK // W


def update_kernel(me_ref, maps_ref, front_ref, l_ref, w_ref, parts_ref, flag_ref, out_ref, list_ref):
    s = pl.program_id(0)
    me = me_ref[0]
    groups = parts_ref.shape[0]
    rows = pl.ds(pl.multiple_of(s * CHUNK, CHUNK), CHUNK)

    @pl.when(s == 0)
    def _():
        count = jnp.int32(0)
        for g in range(groups):
            mine = maps_ref[g, lax.rem(me, 8)] == me
            list_ref[count] = g
            count = count + mine.astype(jnp.int32)
        list_ref[groups] = count

    @pl.when(me < PANELS)
    def _():
        out_ref[...] = l_ref[jnp.minimum(me, PANELS - 1), rows, :].astype(F32)

    @pl.when(me >= PANELS)
    def _():
        left = jnp.concatenate([l_ref[k, rows, :] for k in range(PANELS)], axis=1)
        out_ref[...] = front_ref[rows, :] - jnp.dot(left, w_ref[...], preferred_element_type=F32)

        def add(n, carry):
            g = list_ref[n]
            for i in range(8):
                block = maps_ref[g, i] - s * SPAN

                @pl.when((block >= 0) & (block < SPAN))
                def _():
                    at = pl.ds(pl.multiple_of(block * W, W), W)
                    out_ref[at, :] += parts_ref[g, PACK + i * W : PACK + (i + 1) * W, :].astype(F32)

            return carry

        lax.fori_loop(0, list_ref[groups], add, 0)

        @pl.when(lax.div(me, SPAN) == s)
        def _():
            at = pl.ds(pl.multiple_of(lax.rem(me, SPAN) * W, W), W)
            row = lax.broadcasted_iota(jnp.int32, (W, W), 0)
            col = lax.broadcasted_iota(jnp.int32, (W, W), 1)
            out_ref[at, :] += jnp.where(row == col, flag_ref[...].astype(F32), 0.0)

        @pl.when(s == 0)
        def _():
            out_ref[:LEAD, :] = jnp.zeros((LEAD, W), F32)


def update(me, maps, front, all_l, w, parts, flags):
    order = front.shape[0]
    vmem = pl.BlockSpec(memory_space=pltpu.VMEM)
    smem = pl.BlockSpec(memory_space=pltpu.SMEM)
    return pl.pallas_call(
        update_kernel,
        out_shape=jax.ShapeDtypeStruct((order, W), F32),
        grid=(order // CHUNK,),
        in_specs=[smem, smem, vmem, vmem, vmem, vmem, vmem],
        out_specs=pl.BlockSpec((CHUNK, W), lambda s: (s, 0)),
        scratch_shapes=[pltpu.SMEM((parts.shape[0] + 1,), jnp.int32)],
        compiler_params=pltpu.CompilerParams(vmem_limit_bytes=VMEM_UPDATE),
        name="update",
    )(me, maps, front, all_l, w, parts, flags)


def on_device(front, contributions, block_map, pivot_flags):
    which = lax.axis_index(("grp", "col")).reshape(1)
    flags = pivot_flags.reshape(1, W)
    all_l, parts, w, maps = panels(front[:LEAD], contributions, block_map, flags)
    all_l = all_l.reshape(PANELS, front.shape[0], W)
    return update(which, maps, front, all_l, w, parts.reshape(16, ROWS, W), flags)


def solution(mesh):
    return jax.shard_map(
        on_device,
        mesh=mesh,
        in_specs=(
            P(None, ("grp", "col")),
            P("grp", None, "col"),
            P("grp", None),
            P(("grp", "col")),
        ),
        out_specs=P(None, ("grp", "col")),
        check_vma=False,
    )
```

time: 147 us -> 137 us (0.932)
  Pallas kernels: 140 us -> 128 us
  local copies, waits for them, and re-layouts: 0.76 us -> 7.34 us
  other arithmetic: 5.85 us -> 0 us
    pallas_call x1, Pallas kernels: 16.7 us -> 8.82 us  [update(): pl.pallas_call(update_kernel, out_shape=jax.ShapeDtypeStruct((order, W),...]
    unnamed x0 -> x10, local copies, waits for them, and re-layouts: none -> 6.38 us
    pallas_call x3 -> x1, Pallas kernels: 123 us -> 120 us  [panels(): pl.pallas_call(panels_kernel, out_shape=(pltpu.VMEM((PANELS, 4, 4, 4, 2,...]
    convert_element_type x4 -> x0, other arithmetic: 3.15 us -> none  [the longest x1 1.07 us: on_device(): contributions[0].astype(BF16)]
    add x2 -> x0, other arithmetic: 1.71 us -> none  [the longest x1 1.71 us: on_device(): own = front[:LEAD] + jnp.where(at, flags.astype(F32), 0.0)]
where the time goes in v3:
time: 137 us; the launch traced here: 136 us
  Pallas kernels  128 us (93%)
  local copies, waits for them, and re-layouts  7.34 us (5%)
    pallas_call x1, Pallas kernels, panels(): pl.pallas_call(panels_kernel, out_shape=(pltpu.VMEM((PANELS, 4, 4, 4, 2,...  120 us
    pallas_call x1, Pallas kernels, update(): pl.pallas_call(update_kernel, out_shape=jax.ShapeDtypeStruct((order, W),...  8.82 us
    unnamed x10, local copies, waits for them, and re-layouts  6.38 us

profile of v3, /device:TPU:9, one launch (start us, length us, event | category | flops | bytes accessed | tf_op | source)
XLA Modules:
  0.0 135.8 jit_solution(6814793741942351084)
XLA Ops:
  0.0 1.0 slice.3.head_ref
  1.0 0.0 copy-start.1
  1.0 1.0 copy-done.1
  2.0 0.0 copy-start.2
  2.0 0.7 copy-done.2
  2.7 0.0 copy-start.4
  2.7 0.7 copy-done.4
  3.3 119.6 %panels.1 = (bf16[4,4,4,4,2,128,128]{6,5,4,3,2,1,0:T(8,128)(2,1)S(1)}, bf16[4,4,1040,128]{3,2,1,0:T(8,128)(2,1)S(1)}, bf16[512,128]{1,0:T(8,128)(2,1)S(1)}, s32[16,128]{1,0:T(8,128)S(1)}) custom-call(f32[512,128]{1,0:T(8,128)S(1)} %slice.3.head_ref, f32[1,1024,128]{2,1,0:T(8,128)S(1)} %copy-done.1, s32[1,8]{1,0:T(1,128)S(1)} %copy-done.4, s32[1,128]{1,0:T(1,128)S(1)} %bitcast.6), custom_call_target="tpu_custom_call" | custom-call | tf_op jit(solution)/shard_map/panels/pallas_call | solution.py:450
  122.9 0.0 copy-start
  122.9 3.4 %copy-done = f32[16384,128]{1,0:T(8,128)S(1)} copy-done((f32[16384,128]{1,0:T(8,128)S(1)}, f32[16384,128]{1,0:T(8,128)}, u32[]{:S(2)}) %copy-start) | copy-done | bytes 8388632
  126.3 0.0 copy-start.3
  126.3 0.7 copy-done.3
  127.0 8.8 %update.1 = f32[16384,128]{1,0:T(8,128)} custom-call(s32[1]{0:T(128)} %bitcast.me_ref, s32[16,128]{1,0:T(8,128)S(1)} %get-tuple-element.9.maps_ref, f32[16384,128]{1,0:T(8,128)S(1)} %copy-done, bf16[4,16384,128]{2,1,0:T(8,128)(2,1)S(1)} %bitcast.4, bf16[512,128]{1,0:T(8,128)(2,1)S(1)} %get-tuple-element.11.w_ref, bf16[16,1040,128]{2,1,0:T(8,128)(2,1)S(1)} %bitcast.5, ...), custom_call_target="tpu_custom_call" | custom-call | tf_op jit(solution)/shard_map/update/pallas_call | solution.py:539
Async XLA Ops:
  1.0 1.0 copy-start.1
  2.0 0.7 copy-start.2
  2.7 0.7 copy-start.4
  122.9 3.4 %copy-start = (f32[16384,128]{1,0:T(8,128)S(1)}, f32[16384,128]{1,0:T(8,128)}, u32[]{:S(2)}) copy-start(f32[16384,128]{1,0:T(8,128)} %front_ref.1) | copy-start | bytes 25165828
  126.3 0.7 copy-start.3

commit v4 on v3

--- a/solution.py
+++ b/solution.py
@@ -73,7 +73,7 @@
 
     def greet(self):
         barrier = pltpu.get_barrier_semaphore()
-        peers = [self.near(d, s) for d in "xyz" for s in (1, -1)] + [self.partner]
+        peers = [self.near(d, s) for d in "xyz" for s in (1, 2, 3)] + [self.partner]
         for peer in peers:
             pl.semaphore_signal(barrier, inc=1, device_id=peer, device_id_type=MESH)
         pl.semaphore_wait(barrier, len(peers))
@@ -97,7 +97,7 @@
         )
 
 
-def gather_stream(place, wires, view, order, rows, middle, across):
+def gather_stream(place, wires, view, order, rows, middle, across, direct):
     lo, hi = pl.ds(rows[0], middle - rows[0]), pl.ds(middle, rows[1] - middle)
     every = pl.ds(rows[0], rows[1] - rows[0])
     sent = []
@@ -123,6 +123,13 @@
         right, left = place.near(dim, 1), place.near(dim, -1)
         to_right = launch(wires.copy(unit(mine, every), right))
         to_left = launch(wires.copy(unit(mine, every), left))
+        if phase < direct:
+            to_far = launch(wires.copy(unit(mine, every), place.near(dim, 2)))
+            yield
+            to_right.wait_recv()
+            to_left.wait_recv()
+            to_far.wait_recv()
+            continue
         if last:
             launch(wires.copy(unit(mine, every), place.partner), d2d)
         yield
@@ -147,6 +154,45 @@
         copy.wait_send()
 
 
+def straight_bcast(on, r, wires, whole, near, partner=None, other=None):
+    legs = [wires.copy(whole, near(n)) for n in (1, 2, 3)]
+    across = wires.copy(whole, partner) if partner is not None else None
+
+    @pl.when(on & (r == 0))
+    def _():
+        for leg in (legs[1], legs[0], legs[2]):
+            leg.start()
+        if across is not None:
+            across.start()
+
+    yield
+    for n in (1, 2, 3):
+
+        @pl.when(on & (r == n))
+        def _():
+            legs[n - 1].wait_recv()
+            if across is not None:
+                across.start()
+
+    if across is not None:
+        yield
+
+        @pl.when(other)
+        def _():
+            across.wait_recv()
+
+        yield
+
+        @pl.when(on)
+        def _():
+            across.wait_send()
+
+    @pl.when(on & (r == 0))
+    def _():
+        for leg in legs:
+            leg.wait_send()
+
+
 def ring_bcast(on, r, wires, whole, lo, hi, right, left, partner=None, other=None):
     to_right, to_left = wires.copy(whole, right), wires.copy(whole, left)
     on_right, on_left = wires.copy(lo, right), wires.copy(hi, left)
@@ -220,10 +266,10 @@
             next(s, None)
 
 
-TILES = ((4, 2, 2), (3, 3, 2), (4, 2, 2), (3, 2, 3))
+TILES = ((3, 3, 2), (3, 2, 3), (2, 3, 3), (3, 3, 2))
 ORDERS = ("xyz", "yzx", "zxy")
-WIRES = 5 * 10 + 8 * 8 + 8 * 4 + 8 * 4 + 16 * 12
-SLOTS = (2, 5, 8, 11, 14)
+WIRES = 4 * 7 + 5 * 3 + 6 * 2 + 6 * 7 + 3 * 2 + 4 * 6 + 4 * 7 + 15 * 12
+SLOTS = (5, 10, 15)
 
 
 def panels_kernel(
@@ -277,9 +323,9 @@
     def child_view(where, rows):
         return cg_ref.at[where["y"], where["x"], rows, :]
 
-    def child_stream(r0, r1, order):
+    def child_stream(r0, r1, order, direct=1):
         middle = r0 + (r1 - r0 + 16) // 32 * 16
-        return gather_stream(place, wires, child_view, order, (r0, r1), middle, False)
+        return gather_stream(place, wires, child_view, order, (r0, r1), middle, False, direct)
 
     def spread(j):
         first, second = ("x", "y") if j % 2 == 0 else ("y", "x")
@@ -287,12 +333,19 @@
         half = W // 2
         refs = [flead_ref.at[pl.ds(at, size)] for at, size in ((base, W), (base, half), (base + half, half))]
         for dim, on in ((first, low & (place.at[second] == 0)), (second, low)):
-            yield from ring_bcast(on, place.at[dim], wires, *refs, place.near(dim, 1), place.near(dim, -1))
+            if j == 0:
+                yield from straight_bcast(on, place.at[dim], wires, refs[0], lambda n, dim=dim: place.near(dim, n))
+            else:
+                yield from ring_bcast(on, place.at[dim], wires, *refs, place.near(dim, 1), place.near(dim, -1))
 
     def lead_unit(l, k):
         on = place.core == l % 2
         r = lax.rem(z - l // 2 + 4, 4)
         half = W // 2
+        if k < 2:
+            return straight_bcast(
+                on, r, wires, lead_ref.at[l, k], lambda n: place.near("z", n), place.partner, place.core != l % 2
+            )
         refs = [lead_ref.at[l, k], lead_ref.at[l, k, pl.ds(0, half)], lead_ref.at[l, k, pl.ds(half, half)]]
         return ring_bcast(
             on, r, wires, *refs, place.near("z", 1), place.near("z", -1), place.partner, place.core != l % 2
@@ -305,7 +358,7 @@
         r0 = 16 * sum(TILES[k][:p])
         n = TILES[k][p]
         half = (n // 2 if (k + p) % 2 else (n + 1) // 2) * 16
-        return gather_stream(place, wires, view, ORDERS[p], (r0, r0 + 16 * n), r0 + half, True)
+        return gather_stream(place, wires, view, ORDERS[p], (r0, r0 + 16 * n), r0 + half, True, 1)
 
     def first_row(s):
         return PACK + s * W if s else 0
@@ -313,13 +366,13 @@
     a = [
         Round(
             [
-                child_stream(first_row(s), PACK + s * W + 64, "xy"),
-                child_stream(PACK + s * W + 64, PACK + s * W + W, "yx"),
-                spread(s),
+                child_stream(first_row(s), PACK + s * W + 64, "xy", 1 if s else 2),
+                child_stream(PACK + s * W + 64, PACK + s * W + W, "yx", 1 if s else 2),
             ]
         )
         for s in range(PANELS)
     ]
+    f = [Round([spread(s)]) for s in range(PANELS)]
     far = PACK + LEAD
     b = [
         Round([child_stream(far + n * W, far + (n + 1) * W, "xy" if n % 2 == 0 else "yx") for n in (m, m + 1)])
@@ -385,60 +438,37 @@
                 (part.astype(F32) * piv).astype(BF16).astype(F32).T.astype(BF16)
             )
 
-    def join(k):
-        return lambda: assemble(k)
-
-    for s in range(PANELS):
-        a[s]()
-    for s in range(PANELS):
-        a[s]()
-    for work in (a[0], a[0], a[1], a[0], join(0), lead[0], a[1], lead[0], a[2], a[1], lead[0], join(1), lead[0]):
-        work()
-    lead[1]()
-    a[2]()
+    def run(*rounds):
+        for work in rounds:
+            work()
+
+    late = (1, 2, 3)
+
+    def begin(k):
+        assemble(k)
+        lead[k]()
+
+    run(a[0], f[0], *[a[k] for k in late], *[f[k] for k in late])
+    run(a[0], f[0], *[f[k] for k in late], *[a[k] for k in late])
+    run(a[0], f[0])
+    begin(0)
+    run(*[f[k] for k in late], b[0], b[1], lead[0], *[a[k] for k in late], lead[0])
     panel(
         0,
         (
-            (lead[1], a[3]),
-            (lead[1], a[2]),
-            (lead[1], join(2), lead[2]),
-            (a[3], b[0]),
-            (lead[2], a[3]),
+            (*[f[k] for k in late], *[a[k] for k in late], b[0], b[1]),
+            (*[f[k] for k in late], lambda: [begin(k) for k in late]),
+            (lead[1],),
         ),
     )
-    panel(
-        1,
-        (
-            (g[0], lead[2]),
-            (join(3), lead[3], lead[2], b[0]),
-            (g[0], lead[3]),
-            (b[0], g[0]),
-            (lead[3],),
-        ),
-    )
-    panel(
-        2,
-        (
-            (g[0], lead[3], g[1]),
-            (b[0], g[1]),
-            (g[0],),
-            (g[1], b[0], b[1]),
-            (g[0],),
-        ),
-    )
-    panel(
-        3,
-        (
-            (g[2], g[1], b[1]),
-            (g[2], g[0]),
-            (g[1], b[1]),
-            (g[2],),
-            (g[1], b[1]),
-        ),
-    )
-    for work in (g[3], g[2], g[3], g[1], g[3], g[2], b[1], g[3], g[2], g[3], g[2], g[3], g[3]):
-        work()
-    for group in a + b + lead + g:
+    run(lead[1], lead[2], lead[3], g[0])
+    panel(1, ((b[0], b[1]), (g[0], lead[2], lead[3]), (lead[2], lead[3])))
+    run(g[0])
+    panel(2, ((g[1],), (b[0], b[1]), (g[1],)))
+    run(g[0])
+    panel(3, ((g[1],), (g[2],), (g[0],)))
+    run(g[2], g[1], g[3], g[2], g[1], g[3], g[0], g[2], g[3], g[1], g[2], g[3], g[3], g[2], g[3])
+    for group in a + f + b + lead + g:
         for stream in group.streams:
             for _ in stream:
                 pass
@@ -472,6 +502,7 @@
         compiler_params=pltpu.CompilerParams(
             collective_id=0, has_side_effects=True, vmem_limit_bytes=VMEM_PANELS
         ),
+        cost_estimate=pl.CostEstimate(flops=2 * 10**10, bytes_accessed=3 * 2**20, transcendentals=0),
         name="panels",
     )(head, contributions, block_map, flags)
 

time: 137 us -> 106 us (0.77)
  Pallas kernels: 128 us -> 101 us
  local copies, waits for them, and re-layouts: 7.34 us -> 3.32 us
    pallas_call x1, Pallas kernels: 120 us -> 92.4 us  [panels(): pl.pallas_call(panels_kernel, out_shape=(pltpu.VMEM((PANELS, 4, 4, 4, 2,...]
    unnamed x10 -> x8, local copies, waits for them, and re-layouts: 6.38 us -> 2.35 us
where the time goes in v4:
time: 106 us; the launch traced here: 104 us
  Pallas kernels  101 us (95%)
  local copies, waits for them, and re-layouts  3.32 us (3%)
    pallas_call x1, Pallas kernels, panels(): pl.pallas_call(panels_kernel, out_shape=(pltpu.VMEM((PANELS, 4, 4, 4, 2,...  92.4 us
    pallas_call x1, Pallas kernels, update(): pl.pallas_call(update_kernel, out_shape=jax.ShapeDtypeStruct((order, W),...  8.42 us
    unnamed x8, local copies, waits for them, and re-layouts  2.35 us

profile of v4, /device:TPU:9, one launch (start us, length us, event | category | flops | bytes accessed | tf_op | source)
XLA Modules:
  0.0 104.2 jit_solution(15753782406338944805)
XLA Ops:
  0.0 1.0 slice.3.head_ref
  1.0 0.0 copy-start.1
  1.0 0.6 copy-done.1
  1.6 0.0 copy-start.2
  1.6 1.0 copy-done.2
  2.7 0.0 copy-start.3
  2.7 0.7 copy-done.3
  3.3 0.0 copy-start
  3.3 92.4 %panels.1 = (bf16[4,4,4,4,2,128,128]{6,5,4,3,2,1,0:T(8,128)(2,1)S(1)}, bf16[4,4,1040,128]{3,2,1,0:T(8,128)(2,1)S(1)}, bf16[512,128]{1,0:T(8,128)(2,1)S(1)}, s32[16,128]{1,0:T(8,128)S(1)}) custom-call(f32[512,128]{1,0:T(8,128)S(1)} %slice.3.head_ref, f32[1,1024,128]{2,1,0:T(8,128)S(1)} %copy-done.2, s32[1,8]{1,0:T(1,128)S(1)} %copy-done.3, s32[1,128]{1,0:T(1,128)S(1)} %bitcast.6), custom_call_target="tpu_custom_call" | custom-call | flops 20000000000 | bytes 3145728 | tf_op jit(solution)/shard_map/panels/pallas_call | solution.py:480
  95.8 0.0 copy-done
  95.8 8.4 %update.1 = f32[16384,128]{1,0:T(8,128)} custom-call(s32[1]{0:T(128)} %bitcast.me_ref, s32[16,128]{1,0:T(8,128)S(1)} %get-tuple-element.9.maps_ref, f32[16384,128]{1,0:T(8,128)S(1)} %copy-done, bf16[4,16384,128]{2,1,0:T(8,128)(2,1)S(1)} %bitcast.4, bf16[512,128]{1,0:T(8,128)(2,1)S(1)} %get-tuple-element.11.w_ref, bf16[16,1040,128]{2,1,0:T(8,128)(2,1)S(1)} %bitcast.5, ...), custom_call_target="tpu_custom_call" | custom-call | tf_op jit(solution)/shard_map/update/pallas_call | solution.py:570
Async XLA Ops:
  1.0 0.7 copy-start.1
  1.6 1.0 copy-start.2
  2.7 0.7 copy-start.3
  3.3 92.4 %copy-start = (f32[16384,128]{1,0:T(8,128)S(1)}, f32[16384,128]{1,0:T(8,128)}, u32[]{:S(2)}) copy-start(f32[16384,128]{1,0:T(8,128)} %front_ref.1) | copy-start | bytes 25165828

commit v5 on v4

--- a/solution.py
+++ b/solution.py
@@ -456,18 +456,16 @@
     panel(
         0,
         (
-            (*[f[k] for k in late], *[a[k] for k in late], b[0], b[1]),
-            (*[f[k] for k in late], lambda: [begin(k) for k in late]),
-            (lead[1],),
+            (*[f[k] for k in late], *[a[k] for k in late], f[1], lambda: begin(1)),
+            (f[2], f[3], lambda: [begin(k) for k in (2, 3)], b[0], b[1]),
+            (),
         ),
     )
-    run(lead[1], lead[2], lead[3], g[0])
-    panel(1, ((b[0], b[1]), (g[0], lead[2], lead[3]), (lead[2], lead[3])))
-    run(g[0])
-    panel(2, ((g[1],), (b[0], b[1]), (g[1],)))
-    run(g[0])
-    panel(3, ((g[1],), (g[2],), (g[0],)))
-    run(g[2], g[1], g[3], g[2], g[1], g[3], g[0], g[2], g[3], g[1], g[2], g[3], g[3], g[2], g[3])
+    run(lead[1], lead[2], lead[3], lead[1])
+    panel(1, ((b[0], b[1]), (lead[2], lead[3]), (lead[2], lead[3], g[0])))
+    panel(2, ((b[0], b[1]), (g[0],), (g[1],)))
+    panel(3, ((), (g[1],), (g[2], g[0])))
+    run(g[1], g[3], g[2], g[0], g[3], g[2], g[1], g[3], g[0], g[2], g[1], g[3], g[0], g[2], g[3], g[1], g[2], g[3])
     for group in a + f + b + lead + g:
         for stream in group.streams:
             for _ in stream:

time: 106 us -> 102 us (0.962); the launches traced: 104 us -> 102 us
  Pallas kernels: 101 us -> 98.5 us
    pallas_call x1, Pallas kernels: 92.4 us -> 89.1 us  [panels(): pl.pallas_call(panels_kernel, out_shape=(pltpu.VMEM((PANELS, 4, 4, 4, 2,...]
where the time goes in v5:
time: 102 us
  Pallas kernels  98.5 us (97%)
  local copies, waits for them, and re-layouts  3.32 us (3%)
    pallas_call x1, Pallas kernels, panels(): pl.pallas_call(panels_kernel, out_shape=(pltpu.VMEM((PANELS, 4, 4, 4, 2,...  89.1 us
    pallas_call x1, Pallas kernels, update(): pl.pallas_call(update_kernel, out_shape=jax.ShapeDtypeStruct((order, W),...  9.35 us
    unnamed x8, local copies, waits for them, and re-layouts  2.35 us

profile of v5, /device:TPU:9, one launch (start us, length us, event | category | flops | bytes accessed | tf_op | source)
XLA Modules:
  0.0 101.8 jit_solution(8605591308755218993)
XLA Ops:
  0.0 1.0 slice.3.head_ref
  1.0 0.0 copy-start.1
  1.0 0.6 copy-done.1
  1.6 0.0 copy-start.2
  1.6 1.0 %copy-done.2 = f32[1,1024,128]{2,1,0:T(8,128)S(1)} copy-done((f32[1,1024,128]{2,1,0:T(8,128)S(1)}, f32[1,1024,128]{2,1,0:T(8,128)}, u32[]{:S(2)}) %copy-start.2) | copy-done | bytes 524312
  2.7 0.0 copy-start.3
  2.7 0.7 copy-done.3
  3.3 0.0 copy-start
  3.3 89.1 %panels.1 = (bf16[4,4,4,4,2,128,128]{6,5,4,3,2,1,0:T(8,128)(2,1)S(1)}, bf16[4,4,1040,128]{3,2,1,0:T(8,128)(2,1)S(1)}, bf16[512,128]{1,0:T(8,128)(2,1)S(1)}, s32[16,128]{1,0:T(8,128)S(1)}) custom-call(f32[512,128]{1,0:T(8,128)S(1)} %slice.3.head_ref, f32[1,1024,128]{2,1,0:T(8,128)S(1)} %copy-done.2, s32[1,8]{1,0:T(1,128)S(1)} %copy-done.3, s32[1,128]{1,0:T(1,128)S(1)} %bitcast.6), custom_call_target="tpu_custom_call" | custom-call | flops 20000000000 | bytes 3145728 | tf_op jit(solution)/shard_map/panels/pallas_call | solution.py:478
  92.5 0.0 copy-done
  92.5 9.4 %update.1 = f32[16384,128]{1,0:T(8,128)} custom-call(s32[1]{0:T(128)} %bitcast.me_ref, s32[16,128]{1,0:T(8,128)S(1)} %get-tuple-element.9.maps_ref, f32[16384,128]{1,0:T(8,128)S(1)} %copy-done, bf16[4,16384,128]{2,1,0:T(8,128)(2,1)S(1)} %bitcast.4, bf16[512,128]{1,0:T(8,128)(2,1)S(1)} %get-tuple-element.11.w_ref, bf16[16,1040,128]{2,1,0:T(8,128)(2,1)S(1)} %bitcast.5, ...), custom_call_target="tpu_custom_call" | custom-call | tf_op jit(solution)/shard_map/update/pallas_call | solution.py:568
Async XLA Ops:
  1.0 0.7 copy-start.1
  1.6 1.0 %copy-start.2 = (f32[1,1024,128]{2,1,0:T(8,128)S(1)}, f32[1,1024,128]{2,1,0:T(8,128)}, u32[]{:S(2)}) copy-start(f32[1,1024,128]{2,1,0:T(8,128)} %child_ref.1) | copy-start | bytes 1572868
  2.7 0.7 copy-start.3
  3.3 89.2 %copy-start = (f32[16384,128]{1,0:T(8,128)S(1)}, f32[16384,128]{1,0:T(8,128)}, u32[]{:S(2)}) copy-start(f32[16384,128]{1,0:T(8,128)} %front_ref.1) | copy-start | bytes 25165828

commit v6 on v5

--- a/solution.py
+++ b/solution.py
@@ -506,8 +506,8 @@
 
 
 VMEM_PANELS = 12 * 2**20
-VMEM_UPDATE = 12 * 2**20
-CHUNK = 2048
+VMEM_UPDATE = 16 * 2**20
+CHUNK = 4096
 SPAN = CHUNK // W
 
 

time: 102 us -> 101 us (level)
  Pallas kernels: 98.5 us -> 96.9 us
    pallas_call x1, Pallas kernels: 9.35 us -> 7.71 us  [update(): pl.pallas_call(update_kernel, out_shape=jax.ShapeDtypeStruct((order, W),...]
    unnamed x8 -> x10, local copies, waits for them, and re-layouts: 2.35 us -> 2.35 us
where the time goes in v6:
time: 101 us; the launch traced here: 100 us
  Pallas kernels  96.9 us (96%)
  local copies, waits for them, and re-layouts  3.32 us (3%)
    pallas_call x1, Pallas kernels, panels(): pl.pallas_call(panels_kernel, out_shape=(pltpu.VMEM((PANELS, 4, 4, 4, 2,...  89.2 us
    pallas_call x1, Pallas kernels, update(): pl.pallas_call(update_kernel, out_shape=jax.ShapeDtypeStruct((order, W),...  7.71 us
    unnamed x10, local copies, waits for them, and re-layouts  2.35 us

profile of v6, /device:TPU:9, one launch (start us, length us, event | category | flops | bytes accessed | tf_op | source)
XLA Modules:
  0.0 100.2 jit_solution(18375485777311483535)
XLA Ops:
  0.0 1.0 slice.3.head_ref
  1.0 0.0 copy-start.1
  1.0 0.6 copy-done.1
  1.6 0.0 copy-start.3
  1.6 1.0 %copy-done.3 = f32[1,1024,128]{2,1,0:T(8,128)S(1)} copy-done((f32[1,1024,128]{2,1,0:T(8,128)S(1)}, f32[1,1024,128]{2,1,0:T(8,128)}, u32[]{:S(2)}) %copy-start.3) | copy-done | bytes 524312
  2.7 0.0 copy-start.4
  2.7 0.7 copy-done.4
  3.3 0.0 copy-start
  3.3 0.0 copy-start.2
  3.3 89.2 %panels.1 = (bf16[4,4,4,4,2,128,128]{6,5,4,3,2,1,0:T(8,128)(2,1)S(1)}, bf16[4,4,1040,128]{3,2,1,0:T(8,128)(2,1)S(1)}, bf16[512,128]{1,0:T(8,128)(2,1)S(1)}, s32[16,128]{1,0:T(8,128)S(1)}) custom-call(f32[512,128]{1,0:T(8,128)S(1)} %slice.3.head_ref, f32[1,1024,128]{2,1,0:T(8,128)S(1)} %copy-done.3, s32[1,8]{1,0:T(1,128)S(1)} %copy-done.4, s32[1,128]{1,0:T(1,128)S(1)} %bitcast.6), custom_call_target="tpu_custom_call" | custom-call | flops 20000000000 | bytes 3145728 | tf_op jit(solution)/shard_map/panels/pallas_call | solution.py:478
  92.5 0.0 copy-done
  92.5 0.0 copy-done.2
  92.5 7.7 %update.1 = f32[16384,128]{1,0:T(8,128)} custom-call(s32[1]{0:T(128)} %bitcast.me_ref, s32[16,128]{1,0:T(8,128)S(1)} %get-tuple-element.9.maps_ref, f32[16384,128]{1,0:T(8,128)S(1)} %copy-done, bf16[4,16384,128]{2,1,0:T(8,128)(2,1)S(1)} %bitcast.4, bf16[512,128]{1,0:T(8,128)(2,1)S(1)} %get-tuple-element.11.w_ref, bf16[16,1040,128]{2,1,0:T(8,128)(2,1)S(1)} %bitcast.5, ...), custom_call_target="tpu_custom_call" | custom-call | tf_op jit(solution)/shard_map/update/pallas_call | solution.py:568
Async XLA Ops:
  1.0 0.7 copy-start.1
  1.6 1.0 %copy-start.3 = (f32[1,1024,128]{2,1,0:T(8,128)S(1)}, f32[1,1024,128]{2,1,0:T(8,128)}, u32[]{:S(2)}) copy-start(f32[1,1024,128]{2,1,0:T(8,128)} %child_ref.1) | copy-start | bytes 1572868
  2.7 0.7 copy-start.4
  3.3 89.2 %copy-start = (f32[16384,128]{1,0:T(8,128)S(1)}, f32[16384,128]{1,0:T(8,128)}, u32[]{:S(2)}) copy-start(f32[16384,128]{1,0:T(8,128)} %front_ref.1) | copy-start | bytes 25165828
  3.3 89.2 %copy-start.2 = (s32[128]{0:T(128)S(1)}, s32[128]{0:T(128)}, u32[]{:S(2)}) copy-start(s32[128]{0:T(128)} %param.7) | copy-start | bytes 1540
